TPU v7x, 32 devices: a whole 2x2x4 slice. The times are simulated.
32 devices in a mesh: rows: 8 (over z, x), rep: 4 (over y, core).
Axes of the slice: x: 2, y: 2, z: 4, core: 2. Of those that a mesh axis runs over, the one named last changes fastest.
Arguments:
- embeddings: bfloat16 [32768, 1024], P(('rows', 'rep')), may hold values from -0.25 to 0.25
- assignments: int32 [32768], P(('rows', 'rep')), may hold values from 0 to 65535, as said below
- old_centroids: bfloat16 [65536, 1024], P('rows'), may hold values from -0.25 to 0.25
- prior_counts: int32 [65536], P('rows'), may hold values from 1 to 8
Outputs:
- centroids: bfloat16 [65536, 1024], P('rows')
- row_score: float32 [32768], P(('rows', 'rep'))
Inputs may be any that keep to these rules, and one draw needn't show every extreme that they name: Within each device's aligned block of 1024 rows the assignments never fall. Cluster k belongs to owner k // 8192; in every block at most 256 rows belong to one owner, and some owner receives exactly 256 of them.
All inputs are finite; a program needn't handle non-finite values.
Results may differ from a plain program's by a relative error of at most 0.0028.
Values may be sent and summed in bfloat16 or wider, within the bound.
No kernel may reach another device: no remote copies, remote signals or barrier semaphores. Data moves between devices by JAX's collectives and lax.ppermute only.
A program may use at most 128 MiB of HBM per device.

v0:
```python
import jax
import jax.numpy as jnp
from jax import lax
from jax.sharding import PartitionSpec as P


def finalize(sums, counts, old_block, prior_block):
    prior = prior_block.astype(jnp.float32)
    total = prior + counts
    mean = (prior[:, None] * old_block.astype(jnp.float32) + sums) / total[:, None]
    scale = lax.rsqrt(jnp.sum(mean * mean, axis=1, keepdims=True) + 1e-06)
    return ((mean * scale).astype(jnp.bfloat16), (1.0 / total).astype(jnp.bfloat16))


def on_device(embeddings, assignments, old_centroids, prior_counts):
    rows_here = embeddings.shape[0]
    width = embeddings.shape[1]
    owners = lax.axis_size("rows")
    groups = lax.axis_size("rep")
    per_owner = old_centroids.shape[0]
    capacity = 2 * rows_here // owners
    owner_of = assignments // per_owner
    owner_list = jnp.arange(owners, dtype=jnp.int32)
    bounds = owner_list * per_owner
    starts = jnp.sum((assignments[None, :] < bounds[:, None]).astype(jnp.int32), axis=1)
    loads = jnp.sum((owner_of[None, :] == owner_list[:, None]).astype(jnp.int32), axis=1)
    position = jnp.arange(capacity, dtype=jnp.int32)
    source = jnp.clip(starts[:, None] + position[None, :], 0, rows_here - 1)
    live = position[None, :] < loads[:, None]
    outgoing = jnp.where(live[:, :, None], embeddings[source], jnp.zeros((), jnp.bfloat16))
    local_ids = jnp.where(live, assignments[source] - bounds[:, None], -1)
    arrived, arrived_ids = (
        lax.all_to_all(outgoing, "rows", split_axis=0, concat_axis=0, tiled=True),
        lax.all_to_all(local_ids, "rows", split_axis=0, concat_axis=0, tiled=True),
    )
    flat = arrived.reshape(-1, width)
    flat_ids = arrived_ids.reshape(-1)
    onehot = (flat_ids[:, None] == jnp.arange(per_owner, dtype=jnp.int32)[None, :]).astype(
        jnp.bfloat16
    )
    partial_sums = lax.dot_general(
        onehot, flat, (((0,), (0,)), ((), ())), preferred_element_type=jnp.float32
    )
    tally = jnp.sum(onehot, axis=0, dtype=jnp.float32)
    sums, counts = (
        lax.psum_scatter(partial_sums, "rep", scatter_dimension=0, tiled=True),
        lax.psum_scatter(tally, "rep", scatter_dimension=0, tiled=True),
    )
    share = per_owner // groups
    offset = lax.axis_index("rep") * share
    old_part = lax.dynamic_slice_in_dim(old_centroids, offset, share, 0)
    prior_part = lax.dynamic_slice_in_dim(prior_counts, offset, share, 0)
    new_part, weight_part = finalize(sums, counts, old_part, prior_part)
    centroids, weight = (
        lax.all_gather(new_part, "rep", axis=0, tiled=True),
        lax.all_gather(weight_part, "rep", axis=0, tiled=True),
    )
    slot_of = jnp.arange(rows_here, dtype=jnp.int32) - starts[owner_of]
    safe_ids = jnp.clip(arrived_ids, 0, per_owner - 1)
    back_rows = centroids[safe_ids]
    back_weight = weight[safe_ids]
    got_rows, got_weight = (
        lax.all_to_all(back_rows, "rows", split_axis=0, concat_axis=0, tiled=True),
        lax.all_to_all(back_weight, "rows", split_axis=0, concat_axis=0, tiled=True),
    )
    mine = got_rows[owner_of, slot_of].astype(jnp.float32)
    diff = embeddings.astype(jnp.float32) - mine
    dist = jnp.sum(diff * diff, axis=1)
    row_score = got_weight[owner_of, slot_of].astype(jnp.float32) * dist
    return (centroids, row_score)


def solution(mesh):
    placed = (P(("rows", "rep"), None), P(("rows", "rep")), P("rows", None), P("rows"))
    return jax.shard_map(
        on_device,
        mesh=mesh,
        in_specs=placed,
        out_specs=(P("rows", None), P(("rows", "rep"))),
        check_vma=False,
    )
```

profile of v0, /device:TPU:0, one launch (start us, length us, event | category | flops | bytes accessed | tf_op | source)
XLA Modules:
  0.0 691.8 jit_solution(8867352214190596665)
XLA Ops:
  7.2 0.9 convert_reduce_fusion.1
  8.1 0.7 fusion.8
  8.9 5.7 select_select_fusion
  14.8 8.6 %gather_fusion = s32[2048]{0:T(1024)S(1)} fusion(s32[1024]{0:T(1024)S(1)} %copy-done, s32[2048]{0:T(1024)S(1)} %broadcast_clamp_fusion.1), kind=kCustom, calls=%fused_computation | custom fusion | bytes 24576 | tf_op jit(solution)/shard_map/gather | solution.py:31
  23.4 0.7 compare_select_fusion.2
  24.0 7.3 %all-to-all-start = ((s32[8,1,256]{2,1,0:T(1,128)}), s32[8,1,256]{2,1,0:T(1,128)S(1)}, u32[]{:S(2)}, u32[]{:S(2)}) async-start(s32[8,1,256]{2,1,0:T(1,128)} %compare_select_fusion.2), calls=%async_computation | async-start | bytes 16384 | tf_op jit(solution)/shard_map/all_to_all | solution.py:34
  31.4 9.6 %gather_fusion.1 = bf16[2048,1024]{1,0:T(8,128)(2,1)} fusion(bf16[1024,1024]{1,0:T(8,128)(2,1)S(1)} %copy-done.1, s32[2048]{0:T(1024)S(1)} %broadcast_clamp_fusion.1), kind=kCustom, calls=%fused_computation.1 | custom fusion | bytes 8396800 | tf_op jit(solution)/shard_map/gather | solution.py:30
  41.0 3.8 broadcast_select_fusion
  44.9 98.8 %all_to_all.29 = bf16[8,256,1024]{2,1,0:T(8,128)(2,1)S(1)} all-to-all(bf16[8,256,1024]{2,1,0:T(8,128)(2,1)} %broadcast_select_fusion), channel_id=1, replica_groups=mesh['rows'=8,'rep'=4] {'rows'}, dimensions={0} | all-to-all | bytes 8388608 | tf_op jit(solution)/shard_map/all_to_all | solution.py:33
  143.7 39.8 %fusion.1 = f32[8192,1024]{1,0:T(8,128)} fusion(bf16[2048,1024]{1,0:T(8,128)(2,1)S(1)} %bitcast.30, s32[2048]{0:T(1024)S(1)} %bitcast.31), kind=kOutput, calls=%fused_computation.9 | convolution fusion | flops 34376515584 | bytes 37756928 | tf_op jit(solution)/shard_map/dot_general | solution.py:41
  183.5 0.6 copy-done.2
  184.1 0.6 dynamic-slice
  185.4 9.6 %convert_reduce_fusion = f32[8192]{0:T(1024)S(1)} fusion(s32[2048]{0:T(1024)S(1)} %bitcast.32), kind=kLoop, calls=%fused_computation.6 | loop fusion | flops 67100672 | bytes 40960 | tf_op jit(solution)/shard_map/reduce_sum | solution.py:44
  195.0 10.4 %all-reduce = f32[8192]{0:T(1024)S(1)} all-reduce(f32[8192]{0:T(1024)S(1)} %convert_reduce_fusion), channel_id=3, replica_groups=mesh['rows'=8,'rep'=4] {'rep'}, use_global_device_ids=true, to_apply=%region_4.5.clone | all-reduce | flops 8192 | bytes 65536
  205.5 0.7 divide_convert_fusion
  206.2 208.6 %reduce-scatter.2.cloned.1.call-done = f32[2048,1024]{1,0:T(8,128)} async-done(((f32[8192,1024]{1,0:T(8,128)}), f32[2048,1024]{1,0:T(8,128)}) %reduce-scatter.2.cloned.1.call-update) | async-done | bytes 8388624 | tf_op jit(solution)/shard_map/reduce_scatter | solution.py:46
  414.8 5.7 multiply_reduce_fusion
  420.5 2.5 multiply_convert_fusion
  423.0 5.2 all_gather.7
  428.3 13.1 %gather_fusion.2 = bf16[2048]{0:T(1024)(128)(2,1)S(1)} fusion(bf16[8192]{0:T(1024)(128)(2,1)S(1)} %all_gather.7, s32[2048]{0:T(1024)S(1)} %broadcast_clamp_fusion), kind=kCustom, calls=%fused_computation.2 | custom fusion | bytes 16384 | tf_op jit(solution)/shard_map/gather | solution.py:61
  441.9 0.7 reduce
  442.6 0.6 reshape.259
  443.2 5.5 all-to-all-start.2
  448.7 80.4 %all-gather.2.cloned.1.call-done = bf16[8192,1024]{1,0:T(8,128)(2,1)} async-done(((bf16[2048,1024]{1,0:T(8,128)(2,1)}), bf16[8192,1024]{1,0:T(8,128)(2,1)}) %all-gather.2.cloned.1.call-update) | async-done | bytes 16777232 | tf_op jit(solution)/shard_map/all_gather | solution.py:55
  529.1 18.9 %gather_fusion.4 = bf16[2048,1024]{1,0:T(8,128)(2,1)} fusion(bf16[8192,1024]{1,0:T(8,128)(2,1)} %all-gather.2.cloned.1.call-done, s32[2048]{0:T(1024)S(1)} %broadcast_clamp_fusion), kind=kCustom, calls=%fused_computation.4 | custom fusion | bytes 8396800 | tf_op jit(solution)/shard_map/gather | solution.py:60
  548.0 5.5 all-to-all-start.3
  553.5 8.7 %gather_fusion.3 = bf16[1024]{0:T(1024)(128)(2,1)S(1)} fusion(bf16[8,256]{1,0:T(8,128)(2,1)S(1)} %bitcast.25, s32[1024]{0:T(1024)S(1)} %bitcast.26), kind=kCustom, calls=%fused_computation.3 | custom fusion | bytes 12288 | tf_op jit(solution)/shard_map/gather | solution.py:69
  562.3 84.9 %all-to-all-done.3 = bf16[8,256,1024]{2,1,0:T(8,128)(2,1)} async-done(((bf16[8,256,1024]{2,1,0:T(8,128)(2,1)}), bf16[8,256,1024]{2,1,0:T(8,128)(2,1)}, u32[]{:S(2)}, u32[]{:S(2)}) %all-to-all-start.3) | async-done | bytes 4194336 | tf_op jit(solution)/shard_map/all_to_all | solution.py:63
  647.2 21.0 %gather_fusion.5 = bf16[1024,1024]{1,0:T(8,128)(2,1)} fusion(bf16[8,256,1024]{2,1,0:T(8,128)(2,1)} %all-to-all-done.3, s32[1024]{0:T(1024)S(1)} %bitcast.27), kind=kCustom, calls=%fused_computation.5 | custom fusion | bytes 4202496 | tf_op jit(solution)/shard_map/gather | solution.py:66
  668.1 2.3 multiply_reduce_fusion.1
  670.5 0.6 convert_multiply_fusion
  671.1 13.9 %copy.12 = bf16[8192,1024]{1,0:T(8,128)(2,1)} copy(bf16[8192,1024]{1,0:T(8,128)(2,1)} %all-gather.2.cloned.1.call-done) | data formatting | bytes 33554432
  (24 shorter events, 1.0 us)
Async XLA Ops:
  7.2 7.6 %copy-start = (s32[1024]{0:T(1024)S(1)}, s32[1024]{0:T(1024)}, u32[]{:S(2)}) copy-start(s32[1024]{0:T(1024)} %param.5) | copy-start | bytes 12292
  14.8 16.7 %copy-start.1 = (bf16[1024,1024]{1,0:T(8,128)(2,1)S(1)}, bf16[1024,1024]{1,0:T(8,128)(2,1)}, u32[]{:S(2)}) copy-start(bf16[1024,1024]{1,0:T(8,128)(2,1)} %param.4) | copy-start | bytes 6291460
  24.0 20.8 %all-to-all-start = ((s32[8,1,256]{2,1,0:T(1,128)}), s32[8,1,256]{2,1,0:T(1,128)S(1)}, u32[]{:S(2)}, u32[]{:S(2)}) async-start(s32[8,1,256]{2,1,0:T(1,128)} %compare_select_fusion.2), calls=%async_computation | async-start | bytes 16384 | tf_op jit(solution)/shard_map/all_to_all | solution.py:34
  31.3 383.4 %reduce-scatter.2.cloned.1.call-start = ((), (), s32[]{:S(2)}) async-start(), calls=%async_computation.5 | async-start | bytes 41943040 | tf_op jit(solution)/shard_map/reduce_scatter | solution.py:46
  183.5 0.7 copy-start.2
  183.5 345.6 %all-gather.2.cloned.1.call-start = ((), (), s32[]{:S(2)}) async-start(), calls=%async_computation.6 | async-start | bytes 20971520 | tf_op jit(solution)/shard_map/all_gather | solution.py:55
  443.2 104.8 %all-to-all-start.2 = ((bf16[8,2,128]{2,1,0:T(2,128)(2,1)}), bf16[8,2,128]{2,1,0:T(2,128)(2,1)S(1)}, u32[]{:S(2)}, u32[]{:S(2)}) async-start(bf16[8,2,128]{2,1,0:T(2,128)(2,1)} %reshape.259), calls=%async_computation.3 | async-start | bytes 8192 | tf_op jit(solution)/shard_map/all_to_all | solution.py:64
  548.0 99.2 %all-to-all-start.3 = ((bf16[8,256,1024]{2,1,0:T(8,128)(2,1)}), bf16[8,256,1024]{2,1,0:T(8,128)(2,1)}, u32[]{:S(2)}, u32[]{:S(2)}) async-start(bf16[8,256,1024]{2,1,0:T(8,128)(2,1)} %bitcast.29), calls=%async_computation.4 | async-start | bytes 8388608 | tf_op jit(solution)/shard_map/all_to_all | solution.py:63
Sparse Core Ops, SparseCore 0:
  183.6 231.1 reduce-scatter.1
  423.2 105.8 all-gather.1
where the time goes:
time: 693 us; the launch traced here: 692 us
  waiting for transfers between devices  374 us (54%)
  blocking collectives  114 us (16%)
  local copies, waits for them, and re-layouts  96.7 us (14%)
  matrix products  39.8 us (6%)
  other arithmetic  33.7 us (5%)
  starting transfers between devices  18.4 us (3%)
  between operations  14.8 us (2%)
    reduce_scatter x1, waiting for transfers between devices, on_device(): lax.psum_scatter(partial_sums, 'rep', scatter_dimension=0, tiled=True)  209 us
    all_to_all x1, blocking collectives, on_device(): lax.all_to_all(outgoing, 'rows', split_axis=0, concat_axis=0, tiled=True)  98.8 us
    all_to_all x1, waiting for transfers between devices, on_device(): lax.all_to_all(back_rows, 'rows', split_axis=0, concat_axis=0, tiled=True)  84.9 us
    all_gather x1, waiting for transfers between devices, on_device(): lax.all_gather(new_part, 'rep', axis=0, tiled=True)  80.4 us
    dot_general x1, matrix products, on_device(): lax.dot_general(onehot, flat, (((0,), (0,)), ((), ())), preferred_element...  39.8 us
    gather x1, local copies, waits for them, and re-layouts, on_device(): mine = got_rows[owner_of, slot_of].astype(jnp.float32)  21 us
    gather x1, local copies, waits for them, and re-layouts, on_device(): back_rows = centroids[safe_ids]  18.9 us
    unnamed x11, local copies, waits for them, and re-layouts  15.7 us
  transfers between devices with their start and end apart: 5, of which 3 were waited for; matrix products, arithmetic and copies ran while one was open for 10% of the time, Pallas kernels for 0%

commit v1 on v0

v1 whole, which is shorter than its diff:
```python
import jax
import jax.numpy as jnp
from jax import lax
from jax.experimental import pallas as pl
from jax.experimental.pallas import tpu as pltpu
from jax.sharding import PartitionSpec as P


LANES = 128
ROWS = 8
STEP = 8
DIGIT = 256


def chunk_sizes(cap):
    last = max(STEP, cap // 4 // STEP * STEP)
    first = max(STEP, cap * 3 // 8 // STEP * STEP)
    return [first, cap - first - last, last]


def pack_rows(starts, rows3, notes, owners, begins, sizes):
    tail = rows3.shape[1:]
    chunks = len(sizes)
    extra = [notes.shape[1] if notes is not None and c == 0 else 0 for c in range(chunks)]

    def body(starts_ref, rows_ref, *rest):
        if notes is not None:
            notes_ref, rest = rest[0], rest[1:]
        outs, sems = rest[:chunks], rest[chunks]

        def copies(owner):
            found = []
            for c in range(chunks):
                begin = starts_ref[owner] + begins[c]
                found.append((rows_ref.at[pl.ds(begin, sizes[c])], outs[c].at[owner, pl.ds(0, sizes[c])]))
            if notes is not None:
                found.append((notes_ref.at[owner], outs[0].at[owner, pl.ds(sizes[0], extra[0])]))
            return [
                pltpu.make_async_copy(source, target, sems.at[k, owner])
                for k, (source, target) in enumerate(found)
            ]

        def start(owner, _):
            for copy in copies(owner):
                copy.start()

        def wait(owner, _):
            for copy in copies(owner):
                copy.wait()

        lax.fori_loop(0, owners, start, None)
        lax.fori_loop(0, owners, wait, None)

    vmem = pl.BlockSpec(memory_space=pltpu.VMEM)
    return pl.pallas_call(
        body,
        in_specs=[pl.BlockSpec(memory_space=pltpu.SMEM), vmem] + [vmem] * (notes is not None),
        out_specs=[pl.BlockSpec(memory_space=pl.ANY)] * chunks,
        out_shape=[
            jax.ShapeDtypeStruct((owners, sizes[c] + extra[c]) + tail, rows3.dtype) for c in range(chunks)
        ],
        scratch_shapes=[pltpu.SemaphoreType.DMA((chunks + 1, owners))],
        name="pack_rows",
    )(starts, rows3, *([notes] if notes is not None else []))


def update(low, high, ids, prior, inverse, old, parts, owners, groups, sizes, pitches):
    clusters, width = old.shape
    chunks = len(parts)
    slabs = width // LANES
    subs = owners * groups
    tile = ROWS * LANES
    steps = clusters // tile
    trash = clusters * slabs
    offsets = [sum(sizes[:c]) for c in range(chunks)]

    def body(low_ref, high_ref, ids_ref, prior_ref, inverse_ref, old_ref, *rest):
        part_refs = rest[: chunks * groups]
        out_ref, dist_ref, acc = rest[chunks * groups : chunks * groups + 3]
        rows = rest[chunks * groups + 3 : chunks * groups + 3 + chunks]
        square, wide, norms, sems = rest[chunks * groups + 3 + chunks :]
        step = pl.program_id(0)

        def fetch(c, g):
            span = owners * pitches[c] * slabs
            return pltpu.make_async_copy(
                part_refs[c * groups + g], rows[c].at[pl.ds(g * span, span)], sems.at[c, g]
            )

        def picked(c, sub, at):
            base = offsets[c] * subs + sub * sizes[c] + at
            return [ids_ref[base + k] for k in range(STEP)]

        def load(c, sub, at):
            first = pl.multiple_of((sub * pitches[c] + at) * slabs, 2 * slabs)
            return rows[c][pl.ds(first, STEP * slabs), :].astype(jnp.float32)

        def spot(place):
            return pl.ds(place, slabs, stride=ROWS)

        def over_rows(c, sub, visit):
            lo = low_ref[c * subs + sub]
            hi = high_ref[c * subs + sub]
            lax.fori_loop(
                lo // STEP, (hi + STEP - 1) // STEP, lambda i, _: visit(i * STEP), None
            )

        def widen(ref):
            turned = ref[...].T
            for r in range(ROWS):
                wide[r * LANES : (r + 1) * LANES, :] = jnp.broadcast_to(
                    turned[:, r : r + 1], (LANES, LANES)
                )

        def place(first, at, half, j):
            return pl.ds(pl.multiple_of((first + at) * slabs + (half * slabs + j) * ROWS, ROWS), ROWS)

        @pl.when(step == 0)
        def _():
            for c in range(chunks):
                for g in range(groups):
                    fetch(c, g).start()

            def clear(i, _):
                where = pl.ds(pl.multiple_of(i * ROWS * LANES, ROWS * LANES), ROWS * LANES)
                acc[where, :] = jnp.zeros((ROWS * LANES, LANES), jnp.float32)

            lax.fori_loop(0, clusters * slabs // (ROWS * LANES), clear, None)
            acc[pl.ds(trash, ROWS * slabs), :] = jnp.zeros((ROWS * slabs, LANES), jnp.float32)
            for c in range(chunks):
                for g in range(groups):
                    fetch(c, g).wait()

                def add_sub(sub, _, c=c):
                    def add(at):
                        found = picked(c, sub, at)
                        new = load(c, sub, at)
                        was = [acc[spot(k), :] for k in found]
                        marks = [jnp.full((slabs, LANES), k, jnp.int32) for k in found]
                        now = []
                        for k in range(STEP):
                            base = was[k]
                            if k > 0:
                                base = jnp.where(marks[k] == marks[k - 1], now[-1], base)
                            now.append(base + new[k * slabs : (k + 1) * slabs])
                        for k in range(STEP):
                            acc[spot(found[k]), :] = now[k]

                    over_rows(c, sub, add)

                lax.fori_loop(0, subs, add_sub, None)

        first = step * tile
        widen(prior_ref)

        def measure(i, _):
            at = pl.multiple_of(i * 2 * ROWS, 2 * ROWS)
            weights = [wide[pl.ds(at + half * ROWS, ROWS), :] for half in range(2)]
            squares = [[], []]
            for j in range(slabs):
                before = old_ref[pl.ds(at, 2 * ROWS), j * LANES : (j + 1) * LANES].astype(jnp.float32)
                for half in range(2):
                    where = place(first, at, half, j)
                    value = weights[half] * before[half * ROWS : (half + 1) * ROWS] + acc[where, :]
                    acc[where, :] = value
                    squares[half].append(value * value)
            for half in range(2):
                parts = squares[half]
                while len(parts) > 1:
                    parts = [a + b for a, b in zip(parts[::2], parts[1::2])]
                norms[pl.ds(at + half * ROWS, ROWS), :] = parts[0]

        lax.fori_loop(0, tile // (2 * ROWS), measure, None, unroll=4)
        length = jnp.broadcast_to(jnp.sum(norms[...], axis=1, keepdims=True), (tile, LANES))
        widen(inverse_ref)
        factor = wide[...]
        wide[...] = factor * lax.rsqrt(factor * factor * length + 1e-06)

        def finish(i, _):
            at = pl.multiple_of(i * 2 * ROWS, 2 * ROWS)
            factors = [wide[pl.ds(at + half * ROWS, ROWS), :] for half in range(2)]
            for j in range(slabs):
                unit = jnp.concatenate(
                    [acc[place(first, at, half, j), :] * factors[half] for half in range(2)], axis=0
                ).astype(jnp.bfloat16)
                out_ref[pl.ds(at, 2 * ROWS), j * LANES : (j + 1) * LANES] = unit
                back = unit.astype(jnp.float32)
                for half in range(2):
                    acc[place(first, at, half, j), :] = back[half * ROWS : (half + 1) * ROWS]

        lax.fori_loop(0, tile // (2 * ROWS), finish, None, unroll=4)

        @pl.when(step == steps - 1)
        def _():
            for c in range(chunks):

                def score_sub(sub, _, c=c):
                    def score(at):
                        found = picked(c, sub, at)
                        new = load(c, sub, at)
                        for k in range(STEP):
                            gap = new[k * slabs : (k + 1) * slabs] - acc[spot(found[k]), :]
                            square[k * slabs : (k + 1) * slabs, :] = gap * gap
                        total = square[pl.ds(0, STEP, stride=slabs), :]
                        for j in range(1, slabs):
                            total = total + square[pl.ds(j, STEP, stride=slabs), :]
                        where = pl.multiple_of(offsets[c] * owners + sub * sizes[c] + at, STEP)
                        dist_ref[pl.ds(where, STEP), :] = total

                    over_rows(c, sub, score)

                lax.fori_loop(0, owners, score_sub, None)

    smem = pl.BlockSpec(memory_space=pltpu.SMEM)
    own = owners * sum(sizes)
    here = lambda i: (i, 0)
    return pl.pallas_call(
        body,
        grid=(steps,),
        in_specs=[
            smem,
            smem,
            smem,
            pl.BlockSpec((ROWS, LANES), here),
            pl.BlockSpec((ROWS, LANES), here),
            pl.BlockSpec((tile, width), here),
        ]
        + [pl.BlockSpec(memory_space=pl.ANY)] * (chunks * groups),
        out_specs=[pl.BlockSpec((tile, width), here), pl.BlockSpec((own, LANES), lambda i: (0, 0))],
        out_shape=[
            jax.ShapeDtypeStruct((clusters, width), jnp.bfloat16),
            jax.ShapeDtypeStruct((own, LANES), jnp.float32),
        ],
        scratch_shapes=[pltpu.VMEM(((clusters + ROWS) * slabs, LANES), jnp.float32)]
        + [pltpu.VMEM((subs * pitch * slabs, LANES), jnp.bfloat16) for pitch in pitches]
        + [
            pltpu.VMEM((STEP * slabs, LANES), jnp.float32),
            pltpu.VMEM((tile, LANES), jnp.float32),
            pltpu.VMEM((tile, LANES), jnp.float32),
            pltpu.SemaphoreType.DMA((chunks, groups)),
        ],
        compiler_params=pltpu.CompilerParams(
            dimension_semantics=("arbitrary",), vmem_limit_bytes=61 * 1024 * 1024
        ),
        name="update_centroids",
    )(low, high, ids, prior, inverse, old, *[piece for part in parts for piece in part])


def two_level(rel, clusters):
    high = (rel // LANES)[:, None] == jnp.arange(clusters // LANES, dtype=jnp.int32)[None, :]
    low = (rel % LANES)[:, None] == jnp.arange(LANES, dtype=jnp.int32)[None, :]
    return high.astype(jnp.bfloat16), low


def spread(own, groups):
    pieces, hop = [own], groups // 2
    while hop > 0:
        pairs = [(source, source ^ hop) for source in range(groups)]
        more = []
        for piece in pieces:
            more.append(lax.ppermute(piece, "rep", pairs))
        pieces = pieces + more
        hop //= 2
    return pieces


def write_notes(rel, clusters, width, slabs):
    owners, cap = rel.shape
    upper = jnp.where(rel < 0, -1, jnp.where(rel < clusters, rel // DIGIT, DIGIT))
    lower = jnp.where((rel >= 0) & (rel < clusters), rel % DIGIT, 0)
    count = -(-cap // width)
    digits = [
        jnp.pad(part, ((0, 0), (0, count * width - cap))).reshape(owners, count, slabs, LANES)
        for part in (upper, lower)
    ]
    return jnp.concatenate(digits, axis=1).astype(jnp.bfloat16)


def read_notes(notes, cap):
    owners, _ = notes.shape[:2]
    digits = notes.astype(jnp.int32).reshape(owners, 2, -1)[:, :, :cap]
    return digits[:, 0] * DIGIT + digits[:, 1]


def on_device(embeddings, assignments, old_centroids, prior_counts):
    rows_here, width = embeddings.shape
    owners = lax.axis_size("rows")
    groups = lax.axis_size("rep")
    clusters = old_centroids.shape[0]
    assert clusters < DIGIT * DIGIT and groups & (groups - 1) == 0
    cap = 2 * rows_here // owners
    sizes = chunk_sizes(cap)
    chunks = len(sizes)
    begins = [sum(sizes[:c]) for c in range(chunks)]
    slabs = width // LANES

    owner = jnp.arange(owners, dtype=jnp.int32)
    bounds = owner * clusters
    starts = jnp.sum((assignments[None, :] < bounds[:, None]).astype(jnp.int32), axis=1)
    starts = jnp.minimum(starts, rows_here - cap)
    slot_row = (starts[:, None] + jnp.arange(cap, dtype=jnp.int32)[None, :]).reshape(-1)
    row = jnp.arange(rows_here, dtype=jnp.int32)
    slot_ids = jnp.sum(
        jnp.where(slot_row[:, None] == row[None, :], assignments[None, :], 0), axis=1
    ).reshape(owners, cap)
    notes = write_notes(slot_ids - bounds[:, None], clusters, width, slabs)

    rows3 = embeddings.reshape(rows_here, slabs, LANES)
    packed = list(pack_rows(starts, rows3, notes, owners, begins[:1], sizes[:1]))
    packed += list(pack_rows(starts, rows3, None, owners, begins[1:], sizes[1:]))
    pitches = [pack.shape[1] for pack in packed]

    parts = []
    for c in range(chunks):
        came = lax.all_to_all(packed[c], "rows", split_axis=0, concat_axis=0, tiled=True)
        pieces = spread(came, groups)
        if c == 0:
            every = [read_notes(piece[:, sizes[0] :], cap) for piece in pieces]
        parts.append([piece.reshape(owners * pitches[c] * slabs, LANES) for piece in pieces])
    rel = jnp.concatenate(every, axis=0)

    inside = (rel >= 0) & (rel < clusters)
    spots = jnp.where(inside, rel, clusters)
    spots = spots // ROWS * (ROWS * slabs) + spots % ROWS
    split = [rel[:, begins[c] : begins[c] + sizes[c]] for c in range(chunks)]
    spots = jnp.concatenate(
        [spots[:, begins[c] : begins[c] + sizes[c]].reshape(-1) for c in range(chunks)]
    )
    low = jnp.concatenate([jnp.sum((part < 0).astype(jnp.int32), axis=1) for part in split])
    high = jnp.concatenate([jnp.sum((part < clusters).astype(jnp.int32), axis=1) for part in split])

    flat = rel.reshape(-1)
    live = (flat >= 0) & (flat < clusters)
    hot_high, hot_low = two_level(jnp.where(live, flat, -1), clusters)
    counts = lax.dot_general(
        hot_high,
        (hot_low & live[:, None]).astype(jnp.bfloat16),
        (((0,), (0,)), ((), ())),
        preferred_element_type=jnp.float32,
    )
    prior = prior_counts.astype(jnp.float32).reshape(clusters // LANES, LANES)
    inverse = 1.0 / (prior + counts)

    centroids, partial = update(
        low, high, spots, prior, inverse, old_centroids, parts, owners, groups, sizes, pitches
    )

    mine = every[0].reshape(-1)
    mine_live = (mine >= 0) & (mine < clusters)
    my_high, my_low = two_level(jnp.where(mine_live, mine, 0), clusters)
    lanes = lax.dot_general(
        my_high,
        inverse.astype(jnp.bfloat16),
        (((1,), (0,)), ((), ())),
        preferred_element_type=jnp.float32,
    )
    my_weight = jnp.sum(jnp.where(my_low, lanes, 0.0), axis=1)

    dist = jnp.sum(partial, axis=1)
    dist = jnp.concatenate(
        [
            dist[owners * begins[c] : owners * (begins[c] + sizes[c])].reshape(owners, sizes[c])
            for c in range(chunks)
        ],
        axis=1,
    ).reshape(-1)
    scores = jnp.where(mine_live, my_weight * dist, 0.0).reshape(owners, cap)
    got = lax.all_to_all(scores, "rows", split_axis=0, concat_axis=0, tiled=True).reshape(-1)
    row_owner = assignments // clusters
    slot_owner = jnp.repeat(owner, cap)
    match = (slot_row[None, :] == row[:, None]) & (slot_owner[None, :] == row_owner[:, None])
    row_score = jnp.sum(jnp.where(match, got[None, :], 0.0), axis=1)
    return (centroids, row_score)


def solution(mesh):
    placed = (P(("rows", "rep"), None), P(("rows", "rep")), P("rows", None), P("rows"))
    return jax.shard_map(
        on_device,
        mesh=mesh,
        in_specs=placed,
        out_specs=(P("rows", None), P(("rows", "rep"))),
        check_vma=False,
    )
```

time: 693 us -> 264 us (0.38)
  waiting for transfers between devices: 374 us -> 125 us
  local copies, waits for them, and re-layouts: 96.7 us -> 4.43 us
  blocking collectives: 114 us -> 42.2 us
  Pallas kernels: 0 us -> 49.4 us
  matrix products: 39.8 us -> 3.61 us
  other arithmetic: 33.7 us -> 13.7 us
  between operations: 14.8 us -> 0.97 us
    reduce_scatter x1 -> x0, waiting for transfers between devices: 209 us -> none  [on_device(): lax.psum_scatter(partial_sums, 'rep', scatter_dimension=0, tiled=True)]
    gather x7 -> x0, local copies, waits for them, and re-layouts: 80.5 us -> none  [the longest x1 21 us: on_device(): mine = got_rows[owner_of, slot_of].astype(jnp.float32)]
    all_gather x1 -> x0, waiting for transfers between devices: 80.4 us -> none  [on_device(): lax.all_gather(new_part, 'rep', axis=0, tiled=True)]
    ppermute x0 -> x9, waiting for transfers between devices: none -> 64.5 us  [spread(): more.append(lax.ppermute(piece, 'rep', pairs))]
    all_to_all x1, blocking collectives: 98.8 us -> 42.2 us  [on_device(): lax.all_to_all(packed[c], 'rows', split_axis=0, concat_axis=0, tiled=True)]
    pallas_call x0 -> x3, Pallas kernels: none -> 49.4 us  [the longest x1 43.1 us: update(): pl.pallas_call(body, grid=(steps,), in_specs=[smem, smem, smem, pl.BlockS...]
    dot_general x1 -> x2, matrix products: 39.8 us -> 3.61 us  [the longest x1 2.99 us: on_device(): lax.dot_general(hot_high, (hot_low & live[:, None]).astype(jnp.bfloat16),...]
    all_to_all x3, waiting for transfers between devices: 84.9 us -> 60.6 us  [the longest x2 54.1 us: on_device(): lax.all_to_all(packed[c], 'rows', split_axis=0, concat_axis=0, tiled=True)]
  transfers between devices with their start and end apart: 5 -> 12, of which waited for: 3 -> 5; matrix products, arithmetic and copies ran while one was open for 10% -> 4% of each run, Pallas kernels for 0% -> 1%
where the time goes in v1:
time: 264 us; the launch traced here: 263 us
  waiting for transfers between devices  125 us (47%)
  Pallas kernels  49.4 us (19%)
  blocking collectives  42.2 us (16%)
  starting transfers between devices  23.2 us (9%)
  other arithmetic  13.7 us (5%)
  local copies, waits for them, and re-layouts  4.43 us (2%)
  matrix products  3.61 us (1%)
    ppermute x9, waiting for transfers between devices, spread(): more.append(lax.ppermute(piece, 'rep', pairs))  64.5 us
    all_to_all x2, waiting for transfers between devices, on_device(): lax.all_to_all(packed[c], 'rows', split_axis=0, concat_axis=0, tiled=True)  54.1 us
    pallas_call x1, Pallas kernels, update(): pl.pallas_call(body, grid=(steps,), in_specs=[smem, smem, smem, pl.BlockS...  43.1 us
    all_to_all x1, blocking collectives, on_device(): lax.all_to_all(packed[c], 'rows', split_axis=0, concat_axis=0, tiled=True)  42.2 us
    all_to_all x2, starting transfers between devices, on_device(): lax.all_to_all(packed[c], 'rows', split_axis=0, concat_axis=0, tiled=True)  11.5 us
    all_to_all x1, starting transfers between devices, on_device(): lax.all_to_all(scores, 'rows', split_axis=0, concat_axis=0, tiled=True)  7.42 us
    all_to_all x1, waiting for transfers between devices, on_device(): lax.all_to_all(scores, 'rows', split_axis=0, concat_axis=0, tiled=True)  6.5 us
    pallas_call x2, Pallas kernels, pack_rows(): pl.pallas_call(body, in_specs=[pl.BlockSpec(memory_space=pltpu.SMEM), vme...  6.32 us
  transfers between devices with their start and end apart: 12, of which 5 were waited for; matrix products, arithmetic and copies ran while one was open for 4% of the time, Pallas kernels for 1%

profile of v1, /device:TPU:0, one launch (start us, length us, event | category | flops | bytes accessed | tf_op | source)
XLA Modules:
  0.0 262.7 jit_solution(12821433630423786912)
XLA Ops:
  0.6 0.9 convert_reduce_fusion
  1.5 0.5 broadcast_minimum_fusion.starts_ref
  2.0 3.5 %copy.38 = bf16[128,8,8,128]{3,2,1,0:T(8,128)(2,1)} copy(bf16[128,8,8,128]{3,1,2,0:T(8,128)(2,1)} %bitcast.63) | data formatting | bytes 4194304
  5.6 3.4 %pack_rows.3 = (bf16[8,96,8,128]{3,2,1,0:T(8,128)(2,1)}, bf16[8,64,8,128]{3,2,1,0:T(8,128)(2,1)}) custom-call(s32[8]{0:T(128)} %broadcast_minimum_fusion.starts_ref, bf16[1024,8,128]{2,1,0:T(8,128)(2,1)} %bitcast.59), custom_call_target="tpu_custom_call" | custom-call | tf_op jit(solution)/shard_map/pack_rows/pallas_call | solution.py:55
  9.0 7.3 %all-to-all-start.1 = ((bf16[8,96,8,128]{3,2,1,0:T(8,128)(2,1)}), bf16[8,96,8,128]{3,2,1,0:T(8,128)(2,1)S(1)}, u32[]{:S(2)}, u32[]{:S(2)}) async-start(bf16[8,96,8,128]{3,2,1,0:T(8,128)(2,1)} %get-tuple-element.6), calls=%async_computation.1 | async-start | bytes 3145728 | tf_op jit(solution)/shard_map/all_to_all | solution.py:315
  16.4 1.5 select_reduce_fusion.1
  18.1 0.6 pad_maximum_fusion.rest_0_
  18.7 2.9 %pack_rows.2 = bf16[8,98,8,128]{3,2,1,0:T(8,128)(2,1)} custom-call(s32[8]{0:T(128)} %broadcast_minimum_fusion.starts_ref, bf16[1024,8,128]{2,1,0:T(8,128)(2,1)} %bitcast.60, bf16[8,2,8,128]{3,2,1,0:T(8,128)(2,1)} %pad_maximum_fusion.rest_0_), custom_call_target="tpu_custom_call" | custom-call | tf_op jit(solution)/shard_map/pack_rows/pallas_call | solution.py:55
  21.6 31.7 %all-to-all-done.1 = bf16[8,96,8,128]{3,2,1,0:T(8,128)(2,1)S(1)} async-done(((bf16[8,96,8,128]{3,2,1,0:T(8,128)(2,1)}), bf16[8,96,8,128]{3,2,1,0:T(8,128)(2,1)S(1)}, u32[]{:S(2)}, u32[]{:S(2)}) %all-to-all-start.1) | async-done | bytes 1572896 | tf_op jit(solution)/shard_map/all_to_all | solution.py:315
  53.3 42.2 %all_to_all.21 = bf16[8,98,8,128]{3,2,1,0:T(8,128)(2,1)S(1)} all-to-all(bf16[8,98,8,128]{3,2,1,0:T(8,128)(2,1)} %pack_rows.2), channel_id=1, replica_groups=mesh['rows'=8,'rep'=4] {'rows'}, dimensions={0} | all-to-all | bytes 3211264 | tf_op jit(solution)/shard_map/all_to_all | solution.py:315
  95.5 4.2 %all-to-all-start.2 = ((bf16[8,64,8,128]{3,2,1,0:T(8,128)(2,1)}), bf16[8,64,8,128]{3,2,1,0:T(8,128)(2,1)}, u32[]{:S(2)}, u32[]{:S(2)}) async-start(bf16[8,64,8,128]{3,2,1,0:T(8,128)(2,1)} %get-tuple-element.7), calls=%async_computation.2 | async-start | bytes 2097152 | tf_op jit(solution)/shard_map/all_to_all | solution.py:315
  99.8 1.6 collective-permute-start
  101.4 0.5 collective-permute-start.3
  101.9 0.6 convert_bitcast_fusion.prior_ref
  102.5 22.4 %all-to-all-done.2 = bf16[8,64,8,128]{3,2,1,0:T(8,128)(2,1)} async-done(((bf16[8,64,8,128]{3,2,1,0:T(8,128)(2,1)}), bf16[8,64,8,128]{3,2,1,0:T(8,128)(2,1)}, u32[]{:S(2)}, u32[]{:S(2)}) %all-to-all-start.2) | async-done | bytes 1048608 | tf_op jit(solution)/shard_map/all_to_all | solution.py:315
  125.0 1.5 collective-permute-start.6
  126.6 11.4 %collective-permute-done = bf16[8,98,8,128]{3,2,1,0:T(8,128)(2,1)} collective-permute-done((bf16[8,98,8,128]{3,2,1,0:T(8,128)(2,1)S(1)}, bf16[8,98,8,128]{3,2,1,0:T(8,128)(2,1)}, u32[]{:S(2)}, u32[]{:S(2)}) %collective-permute-start) | collective-permute-done | bytes 1605664 | tf_op jit(solution)/shard_map/ppermute | solution.py:261
  138.0 0.8 slice_convert_fusion.2
  138.8 53.1 %collective-permute-done.6 = bf16[8,64,8,128]{3,2,1,0:T(8,128)(2,1)} collective-permute-done((bf16[8,64,8,128]{3,2,1,0:T(8,128)(2,1)}, bf16[8,64,8,128]{3,2,1,0:T(8,128)(2,1)}, u32[]{:S(2)}, u32[]{:S(2)}) %collective-permute-start.6) | collective-permute-done | bytes 1048608 | tf_op jit(solution)/shard_map/ppermute | solution.py:261
  192.5 0.8 slice_convert_fusion.1
  193.4 0.8 slice_convert_fusion
  195.1 0.7 pad_add_fusion.3.high_ref
  195.8 0.6 pad_add_fusion.2.low_ref
  196.3 0.6 pad_add_fusion.1.ids_ref
  197.0 3.0 %fusion.10.inverse_ref = f32[64,128]{1,0:T(8,128)} fusion(s32[8192]{0:T(1024)S(1)} %get-tuple-element.23, pred[8192]{0:T(1024)(128)(4,1)S(1)} %compare_and_fusion, s32[8192]{0:T(1024)S(1)} %get-tuple-element.22, s32[8192]{0:T(1024)S(1)} %copy-done.2), kind=kOutput, calls=%fused_computation.14 | convolution fusion | flops 136863744 | bytes 139264 | tf_op jit(solution)/shard_map/dot_general | solution.py:335
  200.0 43.1 %update_centroids.1 = (bf16[8192,1024]{1,0:T(8,128)(2,1)}, f32[2048,128]{1,0:T(8,128)}) custom-call(s32[96]{0:T(128)} %pad_add_fusion.2.low_ref, s32[96]{0:T(128)} %pad_add_fusion.3.high_ref, s32[8192]{0:T(1024)} %pad_add_fusion.1.ids_ref, f32[64,128]{1,0:T(8,128)} %convert_bitcast_fusion.prior_ref, f32[64,128]{1,0:T(8,128)} %fusion.10.inverse_ref, ...), custom_call_target="tpu_custom_call" | custom-call | tf_op jit(solution)/shard_map/update_centroids/pallas_call | solution.py:217
  243.2 1.6 reduce_sum.111
  245.0 0.6 fusion.6
  245.6 0.7 and_select_fusion
  246.3 7.4 %all-to-all-start.3 = ((f32[8,1,256]{2,1,0:T(1,128)}), f32[8,1,256]{2,1,0:T(1,128)S(1)}, u32[]{:S(2)}, u32[]{:S(2)}) async-start(f32[8,1,256]{2,1,0:T(1,128)} %and_select_fusion), calls=%async_computation.3 | async-start | bytes 16384 | tf_op jit(solution)/shard_map/all_to_all | solution.py:368
  253.8 6.5 %all-to-all-done.3 = f32[8,1,256]{2,1,0:T(1,128)S(1)} async-done(((f32[8,1,256]{2,1,0:T(1,128)}), f32[8,1,256]{2,1,0:T(1,128)S(1)}, u32[]{:S(2)}, u32[]{:S(2)}) %all-to-all-start.3) | async-done | bytes 8224 | tf_op jit(solution)/shard_map/all_to_all | solution.py:368
  260.3 2.5 select_reduce_fusion
  (68 shorter events, 2.2 us)
Async XLA Ops:
  9.0 7.3 %copy-start.5 = (s32[8]{0:T(128)S(1)}, s32[8]{0:T(128)}, u32[]{:S(2)}) copy-start(s32[8]{0:T(128)} %broadcast_minimum_fusion.starts_ref) | copy-start | bytes 100
  9.0 7.4 %copy-start.4 = (s32[1024]{0:T(1024)S(1)}, s32[1024]{0:T(1024)}, u32[]{:S(2)}) copy-start(s32[1024]{0:T(1024)} %param.5) | copy-start | bytes 12292
  9.0 44.3 %all-to-all-start.1 = ((bf16[8,96,8,128]{3,2,1,0:T(8,128)(2,1)}), bf16[8,96,8,128]{3,2,1,0:T(8,128)(2,1)S(1)}, u32[]{:S(2)}, u32[]{:S(2)}) async-start(bf16[8,96,8,128]{3,2,1,0:T(8,128)(2,1)} %get-tuple-element.6), calls=%async_computation.1 | async-start | bytes 3145728 | tf_op jit(solution)/shard_map/all_to_all | solution.py:315
  21.6 80.3 %copy-start.2 = (s32[8192]{0:T(1024)S(1)}, s32[8192]{0:T(1024)}, u32[]{:S(2)}) copy-start(s32[8192]{0:T(1024)} %param.7) | copy-start | bytes 98308
  53.3 138.6 %copy-start.1 = (bf16[8,96,8,128]{3,2,1,0:T(8,128)(2,1)}, bf16[8,96,8,128]{3,2,1,0:T(8,128)(2,1)S(1)}, u32[]{:S(2)}) copy-start(bf16[8,96,8,128]{3,2,1,0:T(8,128)(2,1)S(1)} %all-to-all-done.1) | copy-start | bytes 4718596
  95.5 104.5 %copy-start = (bf16[8,98,8,128]{3,2,1,0:T(8,128)(2,1)}, bf16[8,98,8,128]{3,2,1,0:T(8,128)(2,1)S(1)}, u32[]{:S(2)}) copy-start(bf16[8,98,8,128]{3,2,1,0:T(8,128)(2,1)S(1)} %all_to_all.21) | copy-start | bytes 4816900
  95.5 29.4 %all-to-all-start.2 = ((bf16[8,64,8,128]{3,2,1,0:T(8,128)(2,1)}), bf16[8,64,8,128]{3,2,1,0:T(8,128)(2,1)}, u32[]{:S(2)}, u32[]{:S(2)}) async-start(bf16[8,64,8,128]{3,2,1,0:T(8,128)(2,1)} %get-tuple-element.7), calls=%async_computation.2 | async-start | bytes 2097152 | tf_op jit(solution)/shard_map/all_to_all | solution.py:315
  99.8 38.1 %collective-permute-start = (bf16[8,98,8,128]{3,2,1,0:T(8,128)(2,1)S(1)}, bf16[8,98,8,128]{3,2,1,0:T(8,128)(2,1)}, u32[]{:S(2)}, u32[]{:S(2)}) collective-permute-start(bf16[8,98,8,128]{3,2,1,0:T(8,128)(2,1)S(1)} %all_to_all.21), channel_id=1, source_target_pairs={{0,2},{1,3},{2,0},{3,1},{4,6},{5,7},{6,4},{7,5},{8,10},{9,11},{10,... | collective-permute-start | bytes 4816904 | tf_op jit(solution)/shard_map/ppermute | solution.py:261
  101.4 91.1 %collective-permute-start.1 = (bf16[8,98,8,128]{3,2,1,0:T(8,128)(2,1)S(1)}, bf16[8,98,8,128]{3,2,1,0:T(8,128)(2,1)}, u32[]{:S(2)}, u32[]{:S(2)}) collective-permute-start(bf16[8,98,8,128]{3,2,1,0:T(8,128)(2,1)S(1)} %all_to_all.21), channel_id=1, source_target_pairs={{0,1},{1,0},{2,3},{3,2},{4,5},{5,4},{6,7},{7,6},{8,9},{9,8},{10,11... | collective-permute-start | bytes 4816904 | tf_op jit(solution)/shard_map/ppermute | solution.py:261
  101.4 90.6 %collective-permute-start.3 = (bf16[8,96,8,128]{3,2,1,0:T(8,128)(2,1)S(1)}, bf16[8,96,8,128]{3,2,1,0:T(8,128)(2,1)}, u32[]{:S(2)}, u32[]{:S(2)}) collective-permute-start(bf16[8,96,8,128]{3,2,1,0:T(8,128)(2,1)S(1)} %all-to-all-done.1), channel_id=1, source_target_pairs={{0,2},{1,3},{2,0},{3,1},{4,6},{5,7},{6,4},{7,5},{8,10},{9,11},{10,... | collective-permute-start | bytes 4718600 | tf_op jit(solution)/shard_map/ppermute | solution.py:261
  125.0 67.0 %collective-permute-start.6 = (bf16[8,64,8,128]{3,2,1,0:T(8,128)(2,1)}, bf16[8,64,8,128]{3,2,1,0:T(8,128)(2,1)}, u32[]{:S(2)}, u32[]{:S(2)}) collective-permute-start(bf16[8,64,8,128]{3,2,1,0:T(8,128)(2,1)} %all-to-all-done.2), channel_id=1, source_target_pairs={{0,2},{1,3},{2,0},{3,1},{4,6},{5,7},{6,4},{7,5},{8,10},{9,11},{10,... | collective-permute-start | bytes 3145736 | tf_op jit(solution)/shard_map/ppermute | solution.py:261
  126.5 73.5 %collective-permute-start.7 = (bf16[8,64,8,128]{3,2,1,0:T(8,128)(2,1)}, bf16[8,64,8,128]{3,2,1,0:T(8,128)(2,1)}, u32[]{:S(2)}, u32[]{:S(2)}) collective-permute-start(bf16[8,64,8,128]{3,2,1,0:T(8,128)(2,1)} %all-to-all-done.2), channel_id=1, source_target_pairs={{0,1},{1,0},{2,3},{3,2},{4,5},{5,4},{6,7},{7,6},{8,9},{9,8},{10,11... | collective-permute-start | bytes 3145736 | tf_op jit(solution)/shard_map/ppermute | solution.py:261
  137.9 55.5 %collective-permute-start.2 = (bf16[8,98,8,128]{3,2,1,0:T(8,128)(2,1)}, bf16[8,98,8,128]{3,2,1,0:T(8,128)(2,1)}, u32[]{:S(2)}, u32[]{:S(2)}) collective-permute-start(bf16[8,98,8,128]{3,2,1,0:T(8,128)(2,1)} %collective-permute-done), channel_id=1, source_target_pairs={{0,1},{1,0},{2,3},{3,2},{4,5},{5,4},{6,7},{7,6},{8,9},{9,8},{10,11... | collective-permute-start | bytes 4816904 | tf_op jit(solution)/shard_map/ppermute | solution.py:261
  191.9 8.1 %collective-permute-start.4 = (bf16[8,96,8,128]{3,2,1,0:T(8,128)(2,1)S(1)}, bf16[8,96,8,128]{3,2,1,0:T(8,128)(2,1)}, u32[]{:S(2)}, u32[]{:S(2)}) collective-permute-start(bf16[8,96,8,128]{3,2,1,0:T(8,128)(2,1)S(1)} %all-to-all-done.1), channel_id=1, source_target_pairs={{0,1},{1,0},{2,3},{3,2},{4,5},{5,4},{6,7},{7,6},{8,9},{9,8},{10,11... | collective-permute-start | bytes 4718600 | tf_op jit(solution)/shard_map/ppermute | solution.py:261
  192.0 8.0 %collective-permute-start.8 = (bf16[8,64,8,128]{3,2,1,0:T(8,128)(2,1)}, bf16[8,64,8,128]{3,2,1,0:T(8,128)(2,1)}, u32[]{:S(2)}, u32[]{:S(2)}) collective-permute-start(bf16[8,64,8,128]{3,2,1,0:T(8,128)(2,1)} %collective-permute-done.6), channel_id=1, source_target_pairs={{0,1},{1,0},{2,3},{3,2},{4,5},{5,4},{6,7},{7,6},{8,9},{9,8},{10,11... | collective-permute-start | bytes 3145736 | tf_op jit(solution)/shard_map/ppermute | solution.py:261
  192.5 7.6 %collective-permute-start.5 = (bf16[8,96,8,128]{3,2,1,0:T(8,128)(2,1)}, bf16[8,96,8,128]{3,2,1,0:T(8,128)(2,1)}, u32[]{:S(2)}, u32[]{:S(2)}) collective-permute-start(bf16[8,96,8,128]{3,2,1,0:T(8,128)(2,1)} %collective-permute-done.3), channel_id=1, source_target_pairs={{0,1},{1,0},{2,3},{3,2},{4,5},{5,4},{6,7},{7,6},{8,9},{9,8},{10,11... | collective-permute-start | bytes 4718600 | tf_op jit(solution)/shard_map/ppermute | solution.py:261
  200.0 45.0 %copy-start.3 = (f32[64,128]{1,0:T(8,128)S(1)}, f32[64,128]{1,0:T(8,128)}, u32[]{:S(2)}) copy-start(f32[64,128]{1,0:T(8,128)} %fusion.10.inverse_ref) | copy-start | bytes 98308
  246.3 13.9 %all-to-all-start.3 = ((f32[8,1,256]{2,1,0:T(1,128)}), f32[8,1,256]{2,1,0:T(1,128)S(1)}, u32[]{:S(2)}, u32[]{:S(2)}) async-start(f32[8,1,256]{2,1,0:T(1,128)} %and_select_fusion), calls=%async_computation.3 | async-start | bytes 16384 | tf_op jit(solution)/shard_map/all_to_all | solution.py:368

commit v2 on v1

--- a/solution.py
+++ b/solution.py
@@ -9,13 +9,18 @@
 LANES = 128
 ROWS = 8
 STEP = 8
+PAIR = 2
 DIGIT = 256
 
 
+CHUNKS = 4
+
+
 def chunk_sizes(cap):
-    last = max(STEP, cap // 4 // STEP * STEP)
-    first = max(STEP, cap * 3 // 8 // STEP * STEP)
-    return [first, cap - first - last, last]
+    less = cap // 16 // STEP * STEP
+    last = (cap // CHUNKS - less * (CHUNKS - 1) // 2) // STEP * STEP
+    sizes = [last + less * (CHUNKS - 1 - c) for c in range(CHUNKS)]
+    return [sizes[0] + cap - sum(sizes)] + sizes[1:]
 
 
 def pack_rows(starts, rows3, notes, owners, begins, sizes):
@@ -195,19 +200,29 @@
             for c in range(chunks):
 
                 def score_sub(sub, _, c=c):
-                    def score(at):
-                        found = picked(c, sub, at)
-                        new = load(c, sub, at)
-                        for k in range(STEP):
-                            gap = new[k * slabs : (k + 1) * slabs] - acc[spot(found[k]), :]
-                            square[k * slabs : (k + 1) * slabs, :] = gap * gap
-                        total = square[pl.ds(0, STEP, stride=slabs), :]
-                        for j in range(1, slabs):
-                            total = total + square[pl.ds(j, STEP, stride=slabs), :]
-                        where = pl.multiple_of(offsets[c] * owners + sub * sizes[c] + at, STEP)
-                        dist_ref[pl.ds(where, STEP), :] = total
-
-                    over_rows(c, sub, score)
+                    begin = low_ref[c * subs + sub] // STEP
+                    end = (high_ref[c * subs + sub] + STEP - 1) // STEP
+
+                    def score(i, _):
+                        for lane in range(PAIR):
+                            at = jnp.minimum(begin + i * PAIR + lane, end - 1) * STEP
+                            found = picked(c, sub, at)
+                            new = load(c, sub, at)
+                            gaps = [
+                                new[k * slabs : (k + 1) * slabs] - acc[spot(found[k]), :]
+                                for k in range(STEP)
+                            ]
+                            for k in range(STEP):
+                                square[lane, k * slabs : (k + 1) * slabs, :] = gaps[k] * gaps[k]
+                        for lane in range(PAIR):
+                            at = jnp.minimum(begin + i * PAIR + lane, end - 1) * STEP
+                            terms = [square[lane, pl.ds(j, STEP, stride=slabs), :] for j in range(slabs)]
+                            while len(terms) > 1:
+                                terms = [a + b for a, b in zip(terms[::2], terms[1::2])]
+                            where = pl.multiple_of(offsets[c] * owners + sub * sizes[c] + at, STEP)
+                            dist_ref[pl.ds(where, STEP), :] = terms[0]
+
+                    lax.fori_loop(0, (end - begin + PAIR - 1) // PAIR, score, None)
 
                 lax.fori_loop(0, owners, score_sub, None)
 
@@ -225,7 +240,7 @@
             pl.BlockSpec((ROWS, LANES), here),
             pl.BlockSpec((tile, width), here),
         ]
-        + [pl.BlockSpec(memory_space=pl.ANY)] * (chunks * groups),
+        + [pl.BlockSpec(memory_space=pltpu.HBM)] * (chunks * groups),
         out_specs=[pl.BlockSpec((tile, width), here), pl.BlockSpec((own, LANES), lambda i: (0, 0))],
         out_shape=[
             jax.ShapeDtypeStruct((clusters, width), jnp.bfloat16),
@@ -234,7 +249,7 @@
         scratch_shapes=[pltpu.VMEM(((clusters + ROWS) * slabs, LANES), jnp.float32)]
         + [pltpu.VMEM((subs * pitch * slabs, LANES), jnp.bfloat16) for pitch in pitches]
         + [
-            pltpu.VMEM((STEP * slabs, LANES), jnp.float32),
+            pltpu.VMEM((PAIR, STEP * slabs, LANES), jnp.float32),
             pltpu.VMEM((tile, LANES), jnp.float32),
             pltpu.VMEM((tile, LANES), jnp.float32),
             pltpu.SemaphoreType.DMA((chunks, groups)),
@@ -306,17 +321,18 @@
     notes = write_notes(slot_ids - bounds[:, None], clusters, width, slabs)
 
     rows3 = embeddings.reshape(rows_here, slabs, LANES)
-    packed = list(pack_rows(starts, rows3, notes, owners, begins[:1], sizes[:1]))
-    packed += list(pack_rows(starts, rows3, None, owners, begins[1:], sizes[1:]))
+    packed = list(pack_rows(starts, rows3, None, owners, begins[:1], sizes[:1]))
+    packed += list(pack_rows(starts, rows3, notes, owners, begins[1:], sizes[1:]))
     pitches = [pack.shape[1] for pack in packed]
 
     parts = []
     for c in range(chunks):
         came = lax.all_to_all(packed[c], "rows", split_axis=0, concat_axis=0, tiled=True)
         pieces = spread(came, groups)
-        if c == 0:
-            every = [read_notes(piece[:, sizes[0] :], cap) for piece in pieces]
+        if c == 1:
+            noted = [piece[:, sizes[1] :] for piece in pieces]
         parts.append([piece.reshape(owners * pitches[c] * slabs, LANES) for piece in pieces])
+    every = [read_notes(piece, cap) for piece in noted]
     rel = jnp.concatenate(every, axis=0)
 
     inside = (rel >= 0) & (rel < clusters)
@@ -341,10 +357,6 @@
     prior = prior_counts.astype(jnp.float32).reshape(clusters // LANES, LANES)
     inverse = 1.0 / (prior + counts)
 
-    centroids, partial = update(
-        low, high, spots, prior, inverse, old_centroids, parts, owners, groups, sizes, pitches
-    )
-
     mine = every[0].reshape(-1)
     mine_live = (mine >= 0) & (mine < clusters)
     my_high, my_low = two_level(jnp.where(mine_live, mine, 0), clusters)
@@ -355,6 +367,10 @@
         preferred_element_type=jnp.float32,
     )
     my_weight = jnp.sum(jnp.where(my_low, lanes, 0.0), axis=1)
+
+    centroids, partial = update(
+        low, high, spots, prior, inverse, old_centroids, parts, owners, groups, sizes, pitches
+    )
 
     dist = jnp.sum(partial, axis=1)
     dist = jnp.concatenate(

time: 264 us -> 272 us (1.030)
  blocking collectives: 42.2 us -> 63.2 us
  waiting for transfers between devices: 125 us -> 112 us
    all_to_all x2, waiting for transfers between devices: 54.1 us -> 26 us  [on_device(): lax.all_to_all(packed[c], 'rows', split_axis=0, concat_axis=0, tiled=True)]
    all_to_all x1 -> x2, blocking collectives: 42.2 us -> 63.2 us  [on_device(): lax.all_to_all(packed[c], 'rows', split_axis=0, concat_axis=0, tiled=True)]
    ppermute x9 -> x12, waiting for transfers between devices: 64.5 us -> 79.6 us  [spread(): more.append(lax.ppermute(piece, 'rep', pairs))]
    all_to_all x2, starting transfers between devices: 11.5 us -> 7.78 us  [on_device(): lax.all_to_all(packed[c], 'rows', split_axis=0, concat_axis=0, tiled=True)]
    ppermute x9 -> x12, starting transfers between devices: 4.2 us -> 6.65 us  [spread(): more.append(lax.ppermute(piece, 'rep', pairs))]
  transfers between devices with their start and end apart: 12 -> 15, of which waited for: 5 -> 5; matrix products, arithmetic and copies ran while one was open for 4% -> 3% of each run, Pallas kernels for 1% -> 1%
where the time goes in v2:
time: 272 us; the launch traced here: 271 us
  waiting for transfers between devices  112 us (41%)
  blocking collectives  63.2 us (23%)
  Pallas kernels  49.6 us (18%)
  starting transfers between devices  21.9 us (8%)
  other arithmetic  14.2 us (5%)
  local copies, waits for them, and re-layouts  6.22 us (2%)
  matrix products  2.99 us (1%)
    ppermute x12, waiting for transfers between devices, spread(): more.append(lax.ppermute(piece, 'rep', pairs))  79.6 us
    all_to_all x2, blocking collectives, on_device(): lax.all_to_all(packed[c], 'rows', split_axis=0, concat_axis=0, tiled=True)  63.2 us
    pallas_call x1, Pallas kernels, update(): pl.pallas_call(body, grid=(steps,), in_specs=[smem, smem, smem, pl.BlockS...  43.2 us
    all_to_all x2, waiting for transfers between devices, on_device(): lax.all_to_all(packed[c], 'rows', split_axis=0, concat_axis=0, tiled=True)  26 us
    all_to_all x2, starting transfers between devices, on_device(): lax.all_to_all(packed[c], 'rows', split_axis=0, concat_axis=0, tiled=True)  7.78 us
    all_to_all x1, starting transfers between devices, on_device(): lax.all_to_all(scores, 'rows', split_axis=0, concat_axis=0, tiled=True)  7.5 us
    ppermute x12, starting transfers between devices, spread(): more.append(lax.ppermute(piece, 'rep', pairs))  6.65 us
    all_to_all x1, waiting for transfers between devices, on_device(): lax.all_to_all(scores, 'rows', split_axis=0, concat_axis=0, tiled=True)  6.5 us
  transfers between devices with their start and end apart: 15, of which 5 were waited for; matrix products, arithmetic and copies ran while one was open for 3% of the time, Pallas kernels for 1%

profile of v2, /device:TPU:0, one launch (start us, length us, event | category | flops | bytes accessed | tf_op | source)
XLA Modules:
  0.0 271.2 jit_solution(5256564847821898101)
XLA Ops:
  0.6 0.9 convert_reduce_fusion
  1.6 2.2 select_reduce_fusion.1
  4.0 3.5 %copy.38 = bf16[128,8,8,128]{3,2,1,0:T(8,128)(2,1)} copy(bf16[128,8,8,128]{3,1,2,0:T(8,128)(2,1)} %bitcast.68) | data formatting | bytes 4194304
  7.5 0.6 pad_maximum_fusion.rest_0_
  8.1 3.4 %pack_rows.2 = (bf16[8,74,8,128]{3,2,1,0:T(8,128)(2,1)}, bf16[8,56,8,128]{3,2,1,0:T(8,128)(2,1)}, bf16[8,40,8,128]{3,2,1,0:T(8,128)(2,1)}) custom-call(s32[8]{0:T(128)} %copy-done.10, bf16[1024,8,128]{2,1,0:T(8,128)(2,1)} %bitcast.63, bf16[8,2,8,128]{3,2,1,0:T(8,128)(2,1)} %pad_maximum_fusion.rest_0_), custom_call_target="tpu_custom_call" | custom-call | tf_op jit(solution)/shard_map/pack_rows/pallas_call | solution.py:60
  11.6 25.0 %all_to_all.26 = bf16[8,40,8,128]{3,2,1,0:T(8,128)(2,1)S(1)} all-to-all(bf16[8,40,8,128]{3,2,1,0:T(8,128)(2,1)} %get-tuple-element.9), channel_id=1, replica_groups=mesh['rows'=8,'rep'=4] {'rows'}, dimensions={0} | all-to-all | bytes 1310720 | tf_op jit(solution)/shard_map/all_to_all | solution.py:330
  36.5 3.6 %all-to-all-start = ((bf16[8,74,8,128]{3,2,1,0:T(8,128)(2,1)}), bf16[8,74,8,128]{3,2,1,0:T(8,128)(2,1)S(1)}, u32[]{:S(2)}, u32[]{:S(2)}) async-start(bf16[8,74,8,128]{3,2,1,0:T(8,128)(2,1)} %get-tuple-element.7), calls=%async_computation | async-start | bytes 2424832 | tf_op jit(solution)/shard_map/all_to_all | solution.py:330
  40.1 2.9 %pack_rows.3 = bf16[8,88,8,128]{3,2,1,0:T(8,128)(2,1)} custom-call(s32[8]{0:T(128)} %copy-done.10, bf16[1024,8,128]{2,1,0:T(8,128)(2,1)} %bitcast.64), custom_call_target="tpu_custom_call" | custom-call | tf_op jit(solution)/shard_map/pack_rows/pallas_call | solution.py:60
  43.0 26.0 %all-to-all-done = bf16[8,74,8,128]{3,2,1,0:T(8,128)(2,1)S(1)} async-done(((bf16[8,74,8,128]{3,2,1,0:T(8,128)(2,1)}), bf16[8,74,8,128]{3,2,1,0:T(8,128)(2,1)S(1)}, u32[]{:S(2)}, u32[]{:S(2)}) %all-to-all-start) | async-done | bytes 1212448 | tf_op jit(solution)/shard_map/all_to_all | solution.py:330
  69.0 38.2 %all_to_all.27 = bf16[8,88,8,128]{3,2,1,0:T(8,128)(2,1)S(1)} all-to-all(bf16[8,88,8,128]{3,2,1,0:T(8,128)(2,1)} %pack_rows.3), channel_id=1, replica_groups=mesh['rows'=8,'rep'=4] {'rows'}, dimensions={0} | all-to-all | bytes 2883584 | tf_op jit(solution)/shard_map/all_to_all | solution.py:330
  107.2 4.2 %all-to-all-start.2 = ((bf16[8,56,8,128]{3,2,1,0:T(8,128)(2,1)}), bf16[8,56,8,128]{3,2,1,0:T(8,128)(2,1)}, u32[]{:S(2)}, u32[]{:S(2)}) async-start(bf16[8,56,8,128]{3,2,1,0:T(8,128)(2,1)} %get-tuple-element.8), calls=%async_computation.2 | async-start | bytes 1835008 | tf_op jit(solution)/shard_map/all_to_all | solution.py:330
  111.4 1.6 collective-permute-start
  113.0 0.6 convert_bitcast_fusion.prior_ref
  114.6 1.6 collective-permute-start.3
  116.2 25.0 %collective-permute-done = bf16[8,74,8,128]{3,2,1,0:T(8,128)(2,1)} collective-permute-done((bf16[8,74,8,128]{3,2,1,0:T(8,128)(2,1)S(1)}, bf16[8,74,8,128]{3,2,1,0:T(8,128)(2,1)}, u32[]{:S(2)}, u32[]{:S(2)}) %collective-permute-start) | collective-permute-done | bytes 1212448 | tf_op jit(solution)/shard_map/ppermute | solution.py:276
  141.1 0.8 slice_convert_fusion.2
  142.0 1.6 collective-permute-start.6
  143.6 0.8 slice_convert_fusion.1
  144.4 41.6 %collective-permute-done.3 = bf16[8,88,8,128]{3,2,1,0:T(8,128)(2,1)} collective-permute-done((bf16[8,88,8,128]{3,2,1,0:T(8,128)(2,1)S(1)}, bf16[8,88,8,128]{3,2,1,0:T(8,128)(2,1)}, u32[]{:S(2)}, u32[]{:S(2)}) %collective-permute-start.3) | collective-permute-done | bytes 1441824 | tf_op jit(solution)/shard_map/ppermute | solution.py:276
  186.6 0.8 slice_convert_fusion
  188.7 0.7 pad_add_fusion.3.high_ref
  189.4 0.6 pad_add_fusion.1.ids_ref
  190.0 13.0 %collective-permute-done.6 = bf16[8,56,8,128]{3,2,1,0:T(8,128)(2,1)S(1)} collective-permute-done((bf16[8,56,8,128]{3,2,1,0:T(8,128)(2,1)}, bf16[8,56,8,128]{3,2,1,0:T(8,128)(2,1)S(1)}, u32[]{:S(2)}, u32[]{:S(2)}) %collective-permute-start.6) | collective-permute-done | bytes 917536 | tf_op jit(solution)/shard_map/ppermute | solution.py:276
  204.3 2.4 fusion.10.inverse_ref
  206.7 0.6 fusion.6
  207.4 0.9 copy-done.4
  208.7 43.2 %update_centroids.1 = (bf16[8192,1024]{1,0:T(8,128)(2,1)}, f32[2048,128]{1,0:T(8,128)}) custom-call(s32[128]{0:T(128)} %pad_add_fusion.2.low_ref, s32[128]{0:T(128)} %pad_add_fusion.3.high_ref, s32[8192]{0:T(1024)} %pad_add_fusion.1.ids_ref, f32[64,128]{1,0:T(8,128)} %convert_bitcast_fusion.prior_ref, f32[64,128]{1,0:T(8,128)} %copy-done.8, ...), custom_call_target="tpu_custom_call" | custom-call | tf_op jit(solution)/shard_map/update_centroids/pallas_call | solution.py:232
  252.0 1.6 reduce_sum.131
  254.0 0.7 and_select_fusion
  254.7 7.5 %all-to-all-start.4 = ((f32[8,1,256]{2,1,0:T(1,128)}), f32[8,1,256]{2,1,0:T(1,128)S(1)}, u32[]{:S(2)}, u32[]{:S(2)}) async-start(f32[8,1,256]{2,1,0:T(1,128)} %and_select_fusion), calls=%async_computation.4 | async-start | bytes 16384 | tf_op jit(solution)/shard_map/all_to_all | solution.py:384
  262.3 6.5 %all-to-all-done.4 = f32[8,1,256]{2,1,0:T(1,128)S(1)} async-done(((f32[8,1,256]{2,1,0:T(1,128)}), f32[8,1,256]{2,1,0:T(1,128)S(1)}, u32[]{:S(2)}, u32[]{:S(2)}) %all-to-all-start.4) | async-done | bytes 8224 | tf_op jit(solution)/shard_map/all_to_all | solution.py:384
  268.8 2.5 select_reduce_fusion
  (93 shorter events, 5.2 us)
Async XLA Ops:
  1.5 6.0 %copy-start.10 = (s32[8]{0:T(128)}, s32[8]{0:T(128)S(1)}, u32[]{:S(2)}) copy-start(s32[8]{0:T(128)S(1)} %broadcast_minimum_fusion.starts_ref) | copy-start | bytes 100
  36.5 77.7 %copy-start.2 = (bf16[8,40,8,128]{3,2,1,0:T(8,128)(2,1)}, bf16[8,40,8,128]{3,2,1,0:T(8,128)(2,1)S(1)}, u32[]{:S(2)}) copy-start(bf16[8,40,8,128]{3,2,1,0:T(8,128)(2,1)S(1)} %all_to_all.26) | copy-start | bytes 1966084
  36.5 32.5 %all-to-all-start = ((bf16[8,74,8,128]{3,2,1,0:T(8,128)(2,1)}), bf16[8,74,8,128]{3,2,1,0:T(8,128)(2,1)S(1)}, u32[]{:S(2)}, u32[]{:S(2)}) async-start(bf16[8,74,8,128]{3,2,1,0:T(8,128)(2,1)} %get-tuple-element.7), calls=%async_computation | async-start | bytes 2424832 | tf_op jit(solution)/shard_map/all_to_all | solution.py:330
  43.0 70.0 %copy-start.7 = (s32[8192]{0:T(1024)S(1)}, s32[8192]{0:T(1024)}, u32[]{:S(2)}) copy-start(s32[8192]{0:T(1024)} %param.7) | copy-start | bytes 98308
  43.0 70.6 %copy-start.9 = (s32[1024]{0:T(1024)S(1)}, s32[1024]{0:T(1024)}, u32[]{:S(2)}) copy-start(s32[1024]{0:T(1024)} %param.5) | copy-start | bytes 12292
  69.0 45.5 %copy-start.1 = (bf16[8,74,8,128]{3,2,1,0:T(8,128)(2,1)}, bf16[8,74,8,128]{3,2,1,0:T(8,128)(2,1)S(1)}, u32[]{:S(2)}) copy-start(bf16[8,74,8,128]{3,2,1,0:T(8,128)(2,1)S(1)} %all-to-all-done) | copy-start | bytes 3637252
  107.2 99.4 %copy-start = (bf16[8,88,8,128]{3,2,1,0:T(8,128)(2,1)}, bf16[8,88,8,128]{3,2,1,0:T(8,128)(2,1)S(1)}, u32[]{:S(2)}) copy-start(bf16[8,88,8,128]{3,2,1,0:T(8,128)(2,1)S(1)} %all_to_all.27) | copy-start | bytes 4325380
  107.2 34.8 %all-to-all-start.2 = ((bf16[8,56,8,128]{3,2,1,0:T(8,128)(2,1)}), bf16[8,56,8,128]{3,2,1,0:T(8,128)(2,1)}, u32[]{:S(2)}, u32[]{:S(2)}) async-start(bf16[8,56,8,128]{3,2,1,0:T(8,128)(2,1)} %get-tuple-element.8), calls=%async_computation.2 | async-start | bytes 1835008 | tf_op jit(solution)/shard_map/all_to_all | solution.py:330
  111.4 29.7 %collective-permute-start = (bf16[8,74,8,128]{3,2,1,0:T(8,128)(2,1)S(1)}, bf16[8,74,8,128]{3,2,1,0:T(8,128)(2,1)}, u32[]{:S(2)}, u32[]{:S(2)}) collective-permute-start(bf16[8,74,8,128]{3,2,1,0:T(8,128)(2,1)S(1)} %all-to-all-done), channel_id=1, source_target_pairs={{0,2},{1,3},{2,0},{3,1},{4,6},{5,7},{6,4},{7,5},{8,10},{9,11},{10,... | collective-permute-start | bytes 3637256 | tf_op jit(solution)/shard_map/ppermute | solution.py:276
  113.6 28.3 %collective-permute-start.1 = (bf16[8,74,8,128]{3,2,1,0:T(8,128)(2,1)S(1)}, bf16[8,74,8,128]{3,2,1,0:T(8,128)(2,1)}, u32[]{:S(2)}, u32[]{:S(2)}) collective-permute-start(bf16[8,74,8,128]{3,2,1,0:T(8,128)(2,1)S(1)} %all-to-all-done), channel_id=1, source_target_pairs={{0,1},{1,0},{2,3},{3,2},{4,5},{5,4},{6,7},{7,6},{8,9},{9,8},{10,11... | collective-permute-start | bytes 3637256 | tf_op jit(solution)/shard_map/ppermute | solution.py:276
  113.6 76.4 %collective-permute-start.9 = (bf16[8,40,8,128]{3,2,1,0:T(8,128)(2,1)S(1)}, bf16[8,40,8,128]{3,2,1,0:T(8,128)(2,1)}, u32[]{:S(2)}, u32[]{:S(2)}) collective-permute-start(bf16[8,40,8,128]{3,2,1,0:T(8,128)(2,1)S(1)} %all_to_all.26), channel_id=1, source_target_pairs={{0,2},{1,3},{2,0},{3,1},{4,6},{5,7},{6,4},{7,5},{8,10},{9,11},{10,... | collective-permute-start | bytes 1966088 | tf_op jit(solution)/shard_map/ppermute | solution.py:276
  114.2 88.8 %collective-permute-start.10 = (bf16[8,40,8,128]{3,2,1,0:T(8,128)(2,1)S(1)}, bf16[8,40,8,128]{3,2,1,0:T(8,128)(2,1)}, u32[]{:S(2)}, u32[]{:S(2)}) collective-permute-start(bf16[8,40,8,128]{3,2,1,0:T(8,128)(2,1)S(1)} %all_to_all.26), channel_id=1, source_target_pairs={{0,1},{1,0},{2,3},{3,2},{4,5},{5,4},{6,7},{7,6},{8,9},{9,8},{10,11... | collective-permute-start | bytes 1966088 | tf_op jit(solution)/shard_map/ppermute | solution.py:276
  114.6 71.5 %collective-permute-start.3 = (bf16[8,88,8,128]{3,2,1,0:T(8,128)(2,1)S(1)}, bf16[8,88,8,128]{3,2,1,0:T(8,128)(2,1)}, u32[]{:S(2)}, u32[]{:S(2)}) collective-permute-start(bf16[8,88,8,128]{3,2,1,0:T(8,128)(2,1)S(1)} %all_to_all.27), channel_id=1, source_target_pairs={{0,2},{1,3},{2,0},{3,1},{4,6},{5,7},{6,4},{7,5},{8,10},{9,11},{10,... | collective-permute-start | bytes 4325384 | tf_op jit(solution)/shard_map/ppermute | solution.py:276
  141.1 44.9 %collective-permute-start.2 = (bf16[8,74,8,128]{3,2,1,0:T(8,128)(2,1)}, bf16[8,74,8,128]{3,2,1,0:T(8,128)(2,1)}, u32[]{:S(2)}, u32[]{:S(2)}) collective-permute-start(bf16[8,74,8,128]{3,2,1,0:T(8,128)(2,1)} %collective-permute-done), channel_id=1, source_target_pairs={{0,1},{1,0},{2,3},{3,2},{4,5},{5,4},{6,7},{7,6},{8,9},{9,8},{10,11... | collective-permute-start | bytes 3637256 | tf_op jit(solution)/shard_map/ppermute | solution.py:276
  142.0 61.1 %collective-permute-start.6 = (bf16[8,56,8,128]{3,2,1,0:T(8,128)(2,1)}, bf16[8,56,8,128]{3,2,1,0:T(8,128)(2,1)S(1)}, u32[]{:S(2)}, u32[]{:S(2)}) collective-permute-start(bf16[8,56,8,128]{3,2,1,0:T(8,128)(2,1)} %all-to-all-done.2), channel_id=1, source_target_pairs={{0,2},{1,3},{2,0},{3,1},{4,6},{5,7},{6,4},{7,5},{8,10},{9,11},{10,... | collective-permute-start | bytes 2752520 | tf_op jit(solution)/shard_map/ppermute | solution.py:276
  186.1 21.3 %collective-permute-start.4 = (bf16[8,88,8,128]{3,2,1,0:T(8,128)(2,1)S(1)}, bf16[8,88,8,128]{3,2,1,0:T(8,128)(2,1)}, u32[]{:S(2)}, u32[]{:S(2)}) collective-permute-start(bf16[8,88,8,128]{3,2,1,0:T(8,128)(2,1)S(1)} %all_to_all.27), channel_id=1, source_target_pairs={{0,1},{1,0},{2,3},{3,2},{4,5},{5,4},{6,7},{7,6},{8,9},{9,8},{10,11... | collective-permute-start | bytes 4325384 | tf_op jit(solution)/shard_map/ppermute | solution.py:276
  186.1 22.2 %collective-permute-start.5 = (bf16[8,88,8,128]{3,2,1,0:T(8,128)(2,1)}, bf16[8,88,8,128]{3,2,1,0:T(8,128)(2,1)}, u32[]{:S(2)}, u32[]{:S(2)}) collective-permute-start(bf16[8,88,8,128]{3,2,1,0:T(8,128)(2,1)} %collective-permute-done.3), channel_id=1, source_target_pairs={{0,1},{1,0},{2,3},{3,2},{4,5},{5,4},{6,7},{7,6},{8,9},{9,8},{10,11... | collective-permute-start | bytes 4325384 | tf_op jit(solution)/shard_map/ppermute | solution.py:276
  190.0 17.3 %collective-permute-start.7 = (bf16[8,56,8,128]{3,2,1,0:T(8,128)(2,1)}, bf16[8,56,8,128]{3,2,1,0:T(8,128)(2,1)S(1)}, u32[]{:S(2)}, u32[]{:S(2)}) collective-permute-start(bf16[8,56,8,128]{3,2,1,0:T(8,128)(2,1)} %all-to-all-done.2), channel_id=1, source_target_pairs={{0,1},{1,0},{2,3},{3,2},{4,5},{5,4},{6,7},{7,6},{8,9},{9,8},{10,11... | collective-permute-start | bytes 2752520 | tf_op jit(solution)/shard_map/ppermute | solution.py:276
  203.0 4.3 %copy-start.3 = (bf16[8,56,8,128]{3,2,1,0:T(8,128)(2,1)}, bf16[8,56,8,128]{3,2,1,0:T(8,128)(2,1)S(1)}, u32[]{:S(2)}) copy-start(bf16[8,56,8,128]{3,2,1,0:T(8,128)(2,1)S(1)} %collective-permute-done.6) | copy-start | bytes 2752516
  203.0 4.3 %collective-permute-start.8 = (bf16[8,56,8,128]{3,2,1,0:T(8,128)(2,1)S(1)}, bf16[8,56,8,128]{3,2,1,0:T(8,128)(2,1)S(1)}, u32[]{:S(2)}, u32[]{:S(2)}) collective-permute-start(bf16[8,56,8,128]{3,2,1,0:T(8,128)(2,1)S(1)} %collective-permute-done.6), channel_id=1, source_target_pairs={{0,1},{1,0},{2,3},{3,2},{4,5},{5,4},{6,7},{7,6},{8,9},{9,8},{10,11... | collective-permute-start | bytes 2752520 | tf_op jit(solution)/shard_map/ppermute | solution.py:276
  203.1 4.2 %collective-permute-start.11 = (bf16[8,40,8,128]{3,2,1,0:T(8,128)(2,1)}, bf16[8,40,8,128]{3,2,1,0:T(8,128)(2,1)S(1)}, u32[]{:S(2)}, u32[]{:S(2)}) collective-permute-start(bf16[8,40,8,128]{3,2,1,0:T(8,128)(2,1)} %collective-permute-done.9), channel_id=1, source_target_pairs={{0,1},{1,0},{2,3},{3,2},{4,5},{5,4},{6,7},{7,6},{8,9},{9,8},{10,11... | collective-permute-start | bytes 1966088 | tf_op jit(solution)/shard_map/ppermute | solution.py:276
  206.6 1.9 copy-start.8
  207.3 1.4 copy-start.6
  207.3 1.0 copy-start.4
  207.3 1.2 copy-start.5
  254.7 14.0 %all-to-all-start.4 = ((f32[8,1,256]{2,1,0:T(1,128)}), f32[8,1,256]{2,1,0:T(1,128)S(1)}, u32[]{:S(2)}, u32[]{:S(2)}) async-start(f32[8,1,256]{2,1,0:T(1,128)} %and_select_fusion), calls=%async_computation.4 | async-start | bytes 16384 | tf_op jit(solution)/shard_map/all_to_all | solution.py:384

commit v3 on v2

--- a/solution.py
+++ b/solution.py
@@ -83,7 +83,7 @@
         part_refs = rest[: chunks * groups]
         out_ref, dist_ref, acc = rest[chunks * groups : chunks * groups + 3]
         rows = rest[chunks * groups + 3 : chunks * groups + 3 + chunks]
-        square, wide, norms, sems = rest[chunks * groups + 3 + chunks :]
+        square, wide, norms, scales, sems = rest[chunks * groups + 3 + chunks :]
         step = pl.program_id(0)
 
         def fetch(c, g):
@@ -99,6 +99,10 @@
         def load(c, sub, at):
             first = pl.multiple_of((sub * pitches[c] + at) * slabs, 2 * slabs)
             return rows[c][pl.ds(first, STEP * slabs), :].astype(jnp.float32)
+
+        def cluster_of(place):
+            shift = (ROWS * slabs).bit_length() - 1
+            return (place >> shift) * ROWS + (place & (ROWS - 1))
 
         def spot(place):
             return pl.ds(place, slabs, stride=ROWS)
@@ -179,19 +183,18 @@
         length = jnp.broadcast_to(jnp.sum(norms[...], axis=1, keepdims=True), (tile, LANES))
         widen(inverse_ref)
         factor = wide[...]
-        wide[...] = factor * lax.rsqrt(factor * factor * length + 1e-06)
+        scales[pl.ds(pl.multiple_of(first, tile), tile), :] = factor * lax.rsqrt(
+            factor * factor * length + 1e-06
+        )
 
         def finish(i, _):
             at = pl.multiple_of(i * 2 * ROWS, 2 * ROWS)
-            factors = [wide[pl.ds(at + half * ROWS, ROWS), :] for half in range(2)]
+            factors = [scales[pl.ds(first + at + half * ROWS, ROWS), :] for half in range(2)]
             for j in range(slabs):
                 unit = jnp.concatenate(
                     [acc[place(first, at, half, j), :] * factors[half] for half in range(2)], axis=0
                 ).astype(jnp.bfloat16)
                 out_ref[pl.ds(at, 2 * ROWS), j * LANES : (j + 1) * LANES] = unit
-                back = unit.astype(jnp.float32)
-                for half in range(2):
-                    acc[place(first, at, half, j), :] = back[half * ROWS : (half + 1) * ROWS]
 
         lax.fori_loop(0, tile // (2 * ROWS), finish, None, unroll=4)
 
@@ -208,10 +211,13 @@
                             at = jnp.minimum(begin + i * PAIR + lane, end - 1) * STEP
                             found = picked(c, sub, at)
                             new = load(c, sub, at)
-                            gaps = [
-                                new[k * slabs : (k + 1) * slabs] - acc[spot(found[k]), :]
-                                for k in range(STEP)
+                            near = [
+                                (acc[spot(k), :] * scales[pl.ds(cluster_of(k), 1), :])
+                                .astype(jnp.bfloat16)
+                                .astype(jnp.float32)
+                                for k in found
                             ]
+                            gaps = [new[k * slabs : (k + 1) * slabs] - near[k] for k in range(STEP)]
                             for k in range(STEP):
                                 square[lane, k * slabs : (k + 1) * slabs, :] = gaps[k] * gaps[k]
                         for lane in range(PAIR):
@@ -241,7 +247,7 @@
             pl.BlockSpec((tile, width), here),
         ]
         + [pl.BlockSpec(memory_space=pltpu.HBM)] * (chunks * groups),
-        out_specs=[pl.BlockSpec((tile, width), here), pl.BlockSpec((own, LANES), lambda i: (0, 0))],
+        out_specs=[pl.BlockSpec((tile, width), here), pl.BlockSpec((own, LANES), lambda i: (0, 0), pipeline_mode=pl.Buffered(1))],
         out_shape=[
             jax.ShapeDtypeStruct((clusters, width), jnp.bfloat16),
             jax.ShapeDtypeStruct((own, LANES), jnp.float32),
@@ -252,10 +258,11 @@
             pltpu.VMEM((PAIR, STEP * slabs, LANES), jnp.float32),
             pltpu.VMEM((tile, LANES), jnp.float32),
             pltpu.VMEM((tile, LANES), jnp.float32),
+            pltpu.VMEM((clusters + ROWS, LANES), jnp.float32),
             pltpu.SemaphoreType.DMA((chunks, groups)),
         ],
         compiler_params=pltpu.CompilerParams(
-            dimension_semantics=("arbitrary",), vmem_limit_bytes=61 * 1024 * 1024
+            dimension_semantics=("arbitrary",), vmem_limit_bytes=63 * 1024 * 1024
         ),
         name="update_centroids",
     )(low, high, ids, prior, inverse, old, *[piece for part in parts for piece in part])

time: 272 us -> 273 us (level)
  no operation moved by 1% of the time
where the time goes in v3:
time: 273 us; the launch traced here: 271 us
  waiting for transfers between devices  112 us (41%)
  blocking collectives  63.2 us (23%)
  Pallas kernels  49.4 us (18%)
  starting transfers between devices  22.3 us (8%)
  other arithmetic  14.2 us (5%)
  local copies, waits for them, and re-layouts  6.22 us (2%)
  matrix products  2.99 us (1%)
    ppermute x12, waiting for transfers between devices, spread(): more.append(lax.ppermute(piece, 'rep', pairs))  79.6 us
    all_to_all x2, blocking collectives, on_device(): lax.all_to_all(packed[c], 'rows', split_axis=0, concat_axis=0, tiled=True)  63.2 us
    pallas_call x1, Pallas kernels, update(): pl.pallas_call(body, grid=(steps,), in_specs=[smem, smem, smem, pl.BlockS...  43.1 us
    all_to_all x2, waiting for transfers between devices, on_device(): lax.all_to_all(packed[c], 'rows', split_axis=0, concat_axis=0, tiled=True)  26 us
    all_to_all x1, starting transfers between devices, on_device(): lax.all_to_all(scores, 'rows', split_axis=0, concat_axis=0, tiled=True)  7.83 us
    all_to_all x2, starting transfers between devices, on_device(): lax.all_to_all(packed[c], 'rows', split_axis=0, concat_axis=0, tiled=True)  7.78 us
    ppermute x12, starting transfers between devices, spread(): more.append(lax.ppermute(piece, 'rep', pairs))  6.65 us
    all_to_all x1, waiting for transfers between devices, on_device(): lax.all_to_all(scores, 'rows', split_axis=0, concat_axis=0, tiled=True)  6.5 us
  transfers between devices with their start and end apart: 15, of which 5 were waited for; matrix products, arithmetic and copies ran while one was open for 3% of the time, Pallas kernels for 1%

profile of v3, /device:TPU:0, one launch (start us, length us, event | category | flops | bytes accessed | tf_op | source)
XLA Modules:
  0.0 271.4 jit_solution(13044218884571009394)
XLA Ops:
  0.6 0.9 convert_reduce_fusion
  1.6 2.2 select_reduce_fusion.1
  4.0 3.5 %copy.38 = bf16[128,8,8,128]{3,2,1,0:T(8,128)(2,1)} copy(bf16[128,8,8,128]{3,1,2,0:T(8,128)(2,1)} %bitcast.68) | data formatting | bytes 4194304
  7.5 0.6 pad_maximum_fusion.rest_0_
  8.1 3.4 %pack_rows.2 = (bf16[8,74,8,128]{3,2,1,0:T(8,128)(2,1)}, bf16[8,56,8,128]{3,2,1,0:T(8,128)(2,1)}, bf16[8,40,8,128]{3,2,1,0:T(8,128)(2,1)}) custom-call(s32[8]{0:T(128)} %copy-done.10, bf16[1024,8,128]{2,1,0:T(8,128)(2,1)} %bitcast.63, bf16[8,2,8,128]{3,2,1,0:T(8,128)(2,1)} %pad_maximum_fusion.rest_0_), custom_call_target="tpu_custom_call" | custom-call | tf_op jit(solution)/shard_map/pack_rows/pallas_call | solution.py:60
  11.6 25.0 %all_to_all.26 = bf16[8,40,8,128]{3,2,1,0:T(8,128)(2,1)S(1)} all-to-all(bf16[8,40,8,128]{3,2,1,0:T(8,128)(2,1)} %get-tuple-element.9), channel_id=1, replica_groups=mesh['rows'=8,'rep'=4] {'rows'}, dimensions={0} | all-to-all | bytes 1310720 | tf_op jit(solution)/shard_map/all_to_all | solution.py:337
  36.5 3.6 %all-to-all-start = ((bf16[8,74,8,128]{3,2,1,0:T(8,128)(2,1)}), bf16[8,74,8,128]{3,2,1,0:T(8,128)(2,1)S(1)}, u32[]{:S(2)}, u32[]{:S(2)}) async-start(bf16[8,74,8,128]{3,2,1,0:T(8,128)(2,1)} %get-tuple-element.7), calls=%async_computation | async-start | bytes 2424832 | tf_op jit(solution)/shard_map/all_to_all | solution.py:337
  40.1 2.9 %pack_rows.3 = bf16[8,88,8,128]{3,2,1,0:T(8,128)(2,1)} custom-call(s32[8]{0:T(128)} %copy-done.10, bf16[1024,8,128]{2,1,0:T(8,128)(2,1)} %bitcast.64), custom_call_target="tpu_custom_call" | custom-call | tf_op jit(solution)/shard_map/pack_rows/pallas_call | solution.py:60
  43.0 26.0 %all-to-all-done = bf16[8,74,8,128]{3,2,1,0:T(8,128)(2,1)S(1)} async-done(((bf16[8,74,8,128]{3,2,1,0:T(8,128)(2,1)}), bf16[8,74,8,128]{3,2,1,0:T(8,128)(2,1)S(1)}, u32[]{:S(2)}, u32[]{:S(2)}) %all-to-all-start) | async-done | bytes 1212448 | tf_op jit(solution)/shard_map/all_to_all | solution.py:337
  69.0 38.2 %all_to_all.27 = bf16[8,88,8,128]{3,2,1,0:T(8,128)(2,1)S(1)} all-to-all(bf16[8,88,8,128]{3,2,1,0:T(8,128)(2,1)} %pack_rows.3), channel_id=1, replica_groups=mesh['rows'=8,'rep'=4] {'rows'}, dimensions={0} | all-to-all | bytes 2883584 | tf_op jit(solution)/shard_map/all_to_all | solution.py:337
  107.2 4.2 %all-to-all-start.2 = ((bf16[8,56,8,128]{3,2,1,0:T(8,128)(2,1)}), bf16[8,56,8,128]{3,2,1,0:T(8,128)(2,1)}, u32[]{:S(2)}, u32[]{:S(2)}) async-start(bf16[8,56,8,128]{3,2,1,0:T(8,128)(2,1)} %get-tuple-element.8), calls=%async_computation.2 | async-start | bytes 1835008 | tf_op jit(solution)/shard_map/all_to_all | solution.py:337
  111.4 1.6 collective-permute-start
  113.0 0.6 convert_bitcast_fusion.prior_ref
  114.6 1.6 collective-permute-start.3
  116.2 25.0 %collective-permute-done = bf16[8,74,8,128]{3,2,1,0:T(8,128)(2,1)} collective-permute-done((bf16[8,74,8,128]{3,2,1,0:T(8,128)(2,1)S(1)}, bf16[8,74,8,128]{3,2,1,0:T(8,128)(2,1)}, u32[]{:S(2)}, u32[]{:S(2)}) %collective-permute-start) | collective-permute-done | bytes 1212448 | tf_op jit(solution)/shard_map/ppermute | solution.py:283
  141.1 0.8 slice_convert_fusion.2
  142.0 1.6 collective-permute-start.6
  143.6 0.8 slice_convert_fusion.1
  144.4 41.6 %collective-permute-done.3 = bf16[8,88,8,128]{3,2,1,0:T(8,128)(2,1)} collective-permute-done((bf16[8,88,8,128]{3,2,1,0:T(8,128)(2,1)S(1)}, bf16[8,88,8,128]{3,2,1,0:T(8,128)(2,1)}, u32[]{:S(2)}, u32[]{:S(2)}) %collective-permute-start.3) | collective-permute-done | bytes 1441824 | tf_op jit(solution)/shard_map/ppermute | solution.py:283
  186.6 0.8 slice_convert_fusion
  188.7 0.7 pad_add_fusion.3.high_ref
  189.4 0.6 pad_add_fusion.1.ids_ref
  190.0 13.0 %collective-permute-done.6 = bf16[8,56,8,128]{3,2,1,0:T(8,128)(2,1)S(1)} collective-permute-done((bf16[8,56,8,128]{3,2,1,0:T(8,128)(2,1)}, bf16[8,56,8,128]{3,2,1,0:T(8,128)(2,1)S(1)}, u32[]{:S(2)}, u32[]{:S(2)}) %collective-permute-start.6) | collective-permute-done | bytes 917536 | tf_op jit(solution)/shard_map/ppermute | solution.py:283
  204.3 2.4 fusion.10.inverse_ref
  206.7 0.6 fusion.6
  207.4 0.9 copy-done.4
  208.7 43.1 %update_centroids.1 = (bf16[8192,1024]{1,0:T(8,128)(2,1)}, f32[2048,128]{1,0:T(8,128)}) custom-call(s32[128]{0:T(128)} %pad_add_fusion.2.low_ref, s32[128]{0:T(128)} %pad_add_fusion.3.high_ref, s32[8192]{0:T(1024)} %pad_add_fusion.1.ids_ref, f32[64,128]{1,0:T(8,128)} %convert_bitcast_fusion.prior_ref, f32[64,128]{1,0:T(8,128)} %copy-done.8, ...), custom_call_target="tpu_custom_call" | custom-call | tf_op jit(solution)/shard_map/update_centroids/pallas_call | solution.py:238
  251.8 1.6 reduce_sum.131
  253.9 0.7 and_select_fusion
  254.6 7.8 %all-to-all-start.4 = ((f32[8,1,256]{2,1,0:T(1,128)}), f32[8,1,256]{2,1,0:T(1,128)S(1)}, u32[]{:S(2)}, u32[]{:S(2)}) async-start(f32[8,1,256]{2,1,0:T(1,128)} %and_select_fusion), calls=%async_computation.4 | async-start | bytes 16384 | tf_op jit(solution)/shard_map/all_to_all | solution.py:391
  262.5 6.5 %all-to-all-done.4 = f32[8,1,256]{2,1,0:T(1,128)S(1)} async-done(((f32[8,1,256]{2,1,0:T(1,128)}), f32[8,1,256]{2,1,0:T(1,128)S(1)}, u32[]{:S(2)}, u32[]{:S(2)}) %all-to-all-start.4) | async-done | bytes 8224 | tf_op jit(solution)/shard_map/all_to_all | solution.py:391
  269.0 2.5 select_reduce_fusion
  (93 shorter events, 5.2 us)
Async XLA Ops:
  1.5 6.0 %copy-start.10 = (s32[8]{0:T(128)}, s32[8]{0:T(128)S(1)}, u32[]{:S(2)}) copy-start(s32[8]{0:T(128)S(1)} %broadcast_minimum_fusion.starts_ref) | copy-start | bytes 100
  36.5 77.7 %copy-start.2 = (bf16[8,40,8,128]{3,2,1,0:T(8,128)(2,1)}, bf16[8,40,8,128]{3,2,1,0:T(8,128)(2,1)S(1)}, u32[]{:S(2)}) copy-start(bf16[8,40,8,128]{3,2,1,0:T(8,128)(2,1)S(1)} %all_to_all.26) | copy-start | bytes 1966084
  36.5 32.5 %all-to-all-start = ((bf16[8,74,8,128]{3,2,1,0:T(8,128)(2,1)}), bf16[8,74,8,128]{3,2,1,0:T(8,128)(2,1)S(1)}, u32[]{:S(2)}, u32[]{:S(2)}) async-start(bf16[8,74,8,128]{3,2,1,0:T(8,128)(2,1)} %get-tuple-element.7), calls=%async_computation | async-start | bytes 2424832 | tf_op jit(solution)/shard_map/all_to_all | solution.py:337
  43.0 70.0 %copy-start.7 = (s32[8192]{0:T(1024)S(1)}, s32[8192]{0:T(1024)}, u32[]{:S(2)}) copy-start(s32[8192]{0:T(1024)} %param.7) | copy-start | bytes 98308
  43.0 70.6 %copy-start.9 = (s32[1024]{0:T(1024)S(1)}, s32[1024]{0:T(1024)}, u32[]{:S(2)}) copy-start(s32[1024]{0:T(1024)} %param.5) | copy-start | bytes 12292
  69.0 45.5 %copy-start.1 = (bf16[8,74,8,128]{3,2,1,0:T(8,128)(2,1)}, bf16[8,74,8,128]{3,2,1,0:T(8,128)(2,1)S(1)}, u32[]{:S(2)}) copy-start(bf16[8,74,8,128]{3,2,1,0:T(8,128)(2,1)S(1)} %all-to-all-done) | copy-start | bytes 3637252
  107.2 99.4 %copy-start = (bf16[8,88,8,128]{3,2,1,0:T(8,128)(2,1)}, bf16[8,88,8,128]{3,2,1,0:T(8,128)(2,1)S(1)}, u32[]{:S(2)}) copy-start(bf16[8,88,8,128]{3,2,1,0:T(8,128)(2,1)S(1)} %all_to_all.27) | copy-start | bytes 4325380
  107.2 34.8 %all-to-all-start.2 = ((bf16[8,56,8,128]{3,2,1,0:T(8,128)(2,1)}), bf16[8,56,8,128]{3,2,1,0:T(8,128)(2,1)}, u32[]{:S(2)}, u32[]{:S(2)}) async-start(bf16[8,56,8,128]{3,2,1,0:T(8,128)(2,1)} %get-tuple-element.8), calls=%async_computation.2 | async-start | bytes 1835008 | tf_op jit(solution)/shard_map/all_to_all | solution.py:337
  111.4 29.7 %collective-permute-start = (bf16[8,74,8,128]{3,2,1,0:T(8,128)(2,1)S(1)}, bf16[8,74,8,128]{3,2,1,0:T(8,128)(2,1)}, u32[]{:S(2)}, u32[]{:S(2)}) collective-permute-start(bf16[8,74,8,128]{3,2,1,0:T(8,128)(2,1)S(1)} %all-to-all-done), channel_id=1, source_target_pairs={{0,2},{1,3},{2,0},{3,1},{4,6},{5,7},{6,4},{7,5},{8,10},{9,11},{10,... | collective-permute-start | bytes 3637256 | tf_op jit(solution)/shard_map/ppermute | solution.py:283
  113.6 28.3 %collective-permute-start.1 = (bf16[8,74,8,128]{3,2,1,0:T(8,128)(2,1)S(1)}, bf16[8,74,8,128]{3,2,1,0:T(8,128)(2,1)}, u32[]{:S(2)}, u32[]{:S(2)}) collective-permute-start(bf16[8,74,8,128]{3,2,1,0:T(8,128)(2,1)S(1)} %all-to-all-done), channel_id=1, source_target_pairs={{0,1},{1,0},{2,3},{3,2},{4,5},{5,4},{6,7},{7,6},{8,9},{9,8},{10,11... | collective-permute-start | bytes 3637256 | tf_op jit(solution)/shard_map/ppermute | solution.py:283
  113.6 76.4 %collective-permute-start.9 = (bf16[8,40,8,128]{3,2,1,0:T(8,128)(2,1)S(1)}, bf16[8,40,8,128]{3,2,1,0:T(8,128)(2,1)}, u32[]{:S(2)}, u32[]{:S(2)}) collective-permute-start(bf16[8,40,8,128]{3,2,1,0:T(8,128)(2,1)S(1)} %all_to_all.26), channel_id=1, source_target_pairs={{0,2},{1,3},{2,0},{3,1},{4,6},{5,7},{6,4},{7,5},{8,10},{9,11},{10,... | collective-permute-start | bytes 1966088 | tf_op jit(solution)/shard_map/ppermute | solution.py:283
  114.2 88.8 %collective-permute-start.10 = (bf16[8,40,8,128]{3,2,1,0:T(8,128)(2,1)S(1)}, bf16[8,40,8,128]{3,2,1,0:T(8,128)(2,1)}, u32[]{:S(2)}, u32[]{:S(2)}) collective-permute-start(bf16[8,40,8,128]{3,2,1,0:T(8,128)(2,1)S(1)} %all_to_all.26), channel_id=1, source_target_pairs={{0,1},{1,0},{2,3},{3,2},{4,5},{5,4},{6,7},{7,6},{8,9},{9,8},{10,11... | collective-permute-start | bytes 1966088 | tf_op jit(solution)/shard_map/ppermute | solution.py:283
  114.6 71.5 %collective-permute-start.3 = (bf16[8,88,8,128]{3,2,1,0:T(8,128)(2,1)S(1)}, bf16[8,88,8,128]{3,2,1,0:T(8,128)(2,1)}, u32[]{:S(2)}, u32[]{:S(2)}) collective-permute-start(bf16[8,88,8,128]{3,2,1,0:T(8,128)(2,1)S(1)} %all_to_all.27), channel_id=1, source_target_pairs={{0,2},{1,3},{2,0},{3,1},{4,6},{5,7},{6,4},{7,5},{8,10},{9,11},{10,... | collective-permute-start | bytes 4325384 | tf_op jit(solution)/shard_map/ppermute | solution.py:283
  141.1 44.9 %collective-permute-start.2 = (bf16[8,74,8,128]{3,2,1,0:T(8,128)(2,1)}, bf16[8,74,8,128]{3,2,1,0:T(8,128)(2,1)}, u32[]{:S(2)}, u32[]{:S(2)}) collective-permute-start(bf16[8,74,8,128]{3,2,1,0:T(8,128)(2,1)} %collective-permute-done), channel_id=1, source_target_pairs={{0,1},{1,0},{2,3},{3,2},{4,5},{5,4},{6,7},{7,6},{8,9},{9,8},{10,11... | collective-permute-start | bytes 3637256 | tf_op jit(solution)/shard_map/ppermute | solution.py:283
  142.0 61.1 %collective-permute-start.6 = (bf16[8,56,8,128]{3,2,1,0:T(8,128)(2,1)}, bf16[8,56,8,128]{3,2,1,0:T(8,128)(2,1)S(1)}, u32[]{:S(2)}, u32[]{:S(2)}) collective-permute-start(bf16[8,56,8,128]{3,2,1,0:T(8,128)(2,1)} %all-to-all-done.2), channel_id=1, source_target_pairs={{0,2},{1,3},{2,0},{3,1},{4,6},{5,7},{6,4},{7,5},{8,10},{9,11},{10,... | collective-permute-start | bytes 2752520 | tf_op jit(solution)/shard_map/ppermute | solution.py:283
  186.1 21.3 %collective-permute-start.4 = (bf16[8,88,8,128]{3,2,1,0:T(8,128)(2,1)S(1)}, bf16[8,88,8,128]{3,2,1,0:T(8,128)(2,1)}, u32[]{:S(2)}, u32[]{:S(2)}) collective-permute-start(bf16[8,88,8,128]{3,2,1,0:T(8,128)(2,1)S(1)} %all_to_all.27), channel_id=1, source_target_pairs={{0,1},{1,0},{2,3},{3,2},{4,5},{5,4},{6,7},{7,6},{8,9},{9,8},{10,11... | collective-permute-start | bytes 4325384 | tf_op jit(solution)/shard_map/ppermute | solution.py:283
  186.1 22.2 %collective-permute-start.5 = (bf16[8,88,8,128]{3,2,1,0:T(8,128)(2,1)}, bf16[8,88,8,128]{3,2,1,0:T(8,128)(2,1)}, u32[]{:S(2)}, u32[]{:S(2)}) collective-permute-start(bf16[8,88,8,128]{3,2,1,0:T(8,128)(2,1)} %collective-permute-done.3), channel_id=1, source_target_pairs={{0,1},{1,0},{2,3},{3,2},{4,5},{5,4},{6,7},{7,6},{8,9},{9,8},{10,11... | collective-permute-start | bytes 4325384 | tf_op jit(solution)/shard_map/ppermute | solution.py:283
  190.0 17.3 %collective-permute-start.7 = (bf16[8,56,8,128]{3,2,1,0:T(8,128)(2,1)}, bf16[8,56,8,128]{3,2,1,0:T(8,128)(2,1)S(1)}, u32[]{:S(2)}, u32[]{:S(2)}) collective-permute-start(bf16[8,56,8,128]{3,2,1,0:T(8,128)(2,1)} %all-to-all-done.2), channel_id=1, source_target_pairs={{0,1},{1,0},{2,3},{3,2},{4,5},{5,4},{6,7},{7,6},{8,9},{9,8},{10,11... | collective-permute-start | bytes 2752520 | tf_op jit(solution)/shard_map/ppermute | solution.py:283
  203.0 4.3 %copy-start.3 = (bf16[8,56,8,128]{3,2,1,0:T(8,128)(2,1)}, bf16[8,56,8,128]{3,2,1,0:T(8,128)(2,1)S(1)}, u32[]{:S(2)}) copy-start(bf16[8,56,8,128]{3,2,1,0:T(8,128)(2,1)S(1)} %collective-permute-done.6) | copy-start | bytes 2752516
  203.0 4.3 %collective-permute-start.8 = (bf16[8,56,8,128]{3,2,1,0:T(8,128)(2,1)S(1)}, bf16[8,56,8,128]{3,2,1,0:T(8,128)(2,1)S(1)}, u32[]{:S(2)}, u32[]{:S(2)}) collective-permute-start(bf16[8,56,8,128]{3,2,1,0:T(8,128)(2,1)S(1)} %collective-permute-done.6), channel_id=1, source_target_pairs={{0,1},{1,0},{2,3},{3,2},{4,5},{5,4},{6,7},{7,6},{8,9},{9,8},{10,11... | collective-permute-start | bytes 2752520 | tf_op jit(solution)/shard_map/ppermute | solution.py:283
  203.1 4.2 %collective-permute-start.11 = (bf16[8,40,8,128]{3,2,1,0:T(8,128)(2,1)}, bf16[8,40,8,128]{3,2,1,0:T(8,128)(2,1)S(1)}, u32[]{:S(2)}, u32[]{:S(2)}) collective-permute-start(bf16[8,40,8,128]{3,2,1,0:T(8,128)(2,1)} %collective-permute-done.9), channel_id=1, source_target_pairs={{0,1},{1,0},{2,3},{3,2},{4,5},{5,4},{6,7},{7,6},{8,9},{9,8},{10,11... | collective-permute-start | bytes 1966088 | tf_op jit(solution)/shard_map/ppermute | solution.py:283
  206.6 1.9 copy-start.8
  207.3 1.4 copy-start.6
  207.3 1.0 copy-start.4
  207.3 1.2 copy-start.5
  254.6 14.4 %all-to-all-start.4 = ((f32[8,1,256]{2,1,0:T(1,128)}), f32[8,1,256]{2,1,0:T(1,128)S(1)}, u32[]{:S(2)}, u32[]{:S(2)}) async-start(f32[8,1,256]{2,1,0:T(1,128)} %and_select_fusion), calls=%async_computation.4 | async-start | bytes 16384 | tf_op jit(solution)/shard_map/all_to_all | solution.py:391
